TPU v7x, 128 devices: a whole 4x4x4 slice. The times are simulated.
128 devices in a mesh: mode: 4 (over y), mesh: 32 (over x, z, core).
Axes of the slice: x: 4, y: 4, z: 4, core: 2. Of those that a mesh axis runs over, the one named last changes fastest.
Arguments:
- velocity: float32 [3, 2, 64, 81920], P(None, None, 'mode', 'mesh'), may hold values from -2.1 to 2.1
- magnetic: float32 [3, 2, 64, 81920], P(None, None, 'mode', 'mesh'), may hold values from -2.1 to 2.1
- leaf_inverse: bfloat16 [64, 640, 128, 128], P('mode', 'mesh'), may hold values from -1 to 2
- leaf_coupling: bfloat16 [64, 128, 81920], P('mode', None, 'mesh'), may hold values from -0.05908203 to 0.05908203
- separator_inverse: bfloat16 [64, 4096, 128], P('mode', 'mesh'), may hold values from -1 to 2
- separator_coupling: bfloat16 [64, 4096, 128], P('mode', 'mesh'), may hold values from -0.26367188 to 0.26367188
- separator_source: float32 [2, 64, 4096], P(None, 'mode', 'mesh'), may hold values from -6 to 6
- front_rows: int32 [32, 2, 128], P('mesh'), may hold values from 0 to 127, each once within a row
Outputs:
- nonlinear: float32 [3, 2, 64, 81920], P(None, None, 'mode', 'mesh')
- azimuthal_field: float32 [2, 64, 81920], P(None, 'mode', 'mesh')
- separator_solution: float32 [2, 64, 4096], P(None, 'mode', 'mesh')
Inputs may be any that keep to these rules, and one draw needn't show every extreme that they name: front_rows[p, 0] and front_rows[p, 1] each hold every number below 128 once.
All inputs are finite; a program needn't handle non-finite values.
Results may differ from a plain program's by a relative error of at most 0.015.
Values may be sent and summed in bfloat16 or wider, within the bound.
A program may use at most 128 MiB of HBM per device.

v0:
```python
import jax
import jax.numpy as jnp
from jax import lax
from jax.sharding import PartitionSpec as P

M = 64
NPHI = 192


dt_step = 0.5


def sent_to_all(x, axis):
    length = lax.axis_size(axis)
    return lax.all_to_all(jnp.broadcast_to(x[None], (length, *x.shape)), axis, 0, 0, tiled=True)


def joined_along(parts, dim):
    parts = jnp.moveaxis(parts, 0, dim)
    shape = parts.shape
    return parts.reshape(*shape[:dim], shape[dim] * shape[dim + 1], *shape[dim + 2 :])


def gather_directly(x, axis, dim):
    parts = sent_to_all(x, axis)
    return joined_along(parts, dim)


def in_one_piece(arrays, axis, dim, along):
    both = jnp.concatenate(arrays, axis=along)
    filled, at, finished = (lax.all_gather(both, axis, axis=dim, tiled=True), 0, [])
    for a in arrays:
        finished.append(lax.slice_in_dim(filled, at, at + a.shape[along], axis=along))
        at += a.shape[along]
    return tuple(finished)


def tables():
    angles = jnp.arange(NPHI, dtype=jnp.int32)[:, None]
    orders = jnp.arange(M, dtype=jnp.int32)[None, :]
    phase = (angles * orders % NPHI).astype(jnp.float32) * (2.0 * jnp.pi / NPHI)
    forward = jnp.stack([jnp.cos(phase), jnp.sin(phase)], axis=1)
    weights = jnp.where(orders == 0, 1.0, 2.0).astype(jnp.float32) / NPHI
    backward = jnp.stack([(jnp.cos(phase) * weights).T, (jnp.sin(phase) * weights).T], axis=0)
    return (forward, backward)


def cross_terms(first, second):
    return jnp.stack(
        [
            first[1] * second[2] - first[2] * second[1],
            first[2] * second[0] - first[0] * second[2],
            first[0] * second[1] - first[1] * second[0],
        ]
    )


def forward_fields(forward, velocity, magnetic):
    return (
        jnp.einsum("kam,camn->ckn", forward, velocity),
        jnp.einsum("kam,camn->ckn", forward, magnetic),
    )


def gather_children(values):
    return gather_directly(values, "mesh", 2)


def gather_parents(values):
    return gather_directly(values, "mesh", 2)


def block_of(whole, index, partitions, sep_rows):
    start = (jnp.clip(index, 0, partitions - 1) * sep_rows).astype(jnp.int32)
    return lax.dynamic_slice_in_dim(whole, start, sep_rows, 2)


def shards(
    velocity,
    magnetic,
    leaf_inverse,
    leaf_coupling,
    separator_inverse,
    separator_coupling,
    separator_source,
    front_rows,
):
    modes_dev = velocity.shape[2]
    nodes_dev = velocity.shape[3]
    forward, backward = tables()
    zeros_phys = jnp.zeros((3, NPHI, nodes_dev), jnp.float32)
    pieces = tuple(
        (
            part.astype(jnp.float32)
            for part in in_one_piece(
                (velocity.astype(jnp.bfloat16), magnetic.astype(jnp.bfloat16)), "mode", 2, 0
            )
        )
    )
    added = forward_fields(forward, pieces[0], pieces[1])
    phys_velocity = zeros_phys + added[0]
    phys_magnetic = zeros_phys + added[1]
    own_rows = lax.dynamic_slice_in_dim(backward, lax.axis_index("mode") * modes_dev, modes_dev, 1)
    nonlinear = jnp.einsum("amk,ckn->camn", own_rows, cross_terms(phys_velocity, phys_magnetic))
    blocks_dev = leaf_inverse.shape[1]
    block_width = leaf_inverse.shape[2]
    sep_rows = separator_source.shape[2]
    source = (magnetic[1] + dt_step * nonlinear[1]).astype(jnp.bfloat16)
    leaf_solved = (
        jnp.einsum(
            "mkij,cmkj->cmki",
            leaf_inverse,
            source.reshape(2, modes_dev, blocks_dev, block_width),
            preferred_element_type=jnp.float32,
        )
        .reshape(2, modes_dev, nodes_dev)
        .astype(jnp.bfloat16)
    )
    row_order = front_rows[0]
    leaf_map = jnp.take(leaf_coupling, row_order[0], axis=1)
    upward_map = jnp.take(separator_coupling, row_order[1], axis=1)
    leaf_update = jnp.einsum(
        "mij,cmj->cmi", leaf_map, leaf_solved, preferred_element_type=jnp.float32
    )
    partitions = lax.axis_size("mesh")
    levels = partitions.bit_length() - 1
    position = lax.axis_index("mesh")
    depth_now = sum(
        [(position % 2**bit_now == 0).astype(jnp.int32) for bit_now in range(1, levels + 1)]
    )
    level_here = depth_now + 1

    def settle(arrived, height, reduced, outgoing):
        fresh = jnp.einsum(
            "mij,cmj->cmi",
            separator_inverse,
            (separator_source - arrived).astype(jnp.bfloat16),
            preferred_element_type=jnp.float32,
        ).astype(jnp.bfloat16)
        sending = jnp.einsum("mij,cmj->cmi", upward_map, fresh, preferred_element_type=jnp.float32)
        active = level_here == height
        return (jnp.where(active, fresh, reduced), jnp.where(active, sending, outgoing))

    reduced = jnp.zeros(separator_source.shape, jnp.bfloat16)
    outgoing = jnp.zeros(separator_source.shape, jnp.float32)
    everyone = gather_children(leaf_update)
    arrived = block_of(everyone, position - 1, partitions, sep_rows) + block_of(
        everyone, position, partitions, sep_rows
    )
    reduced, outgoing = settle(arrived, 1, reduced, outgoing)
    for height in range(2, levels + 1):
        gap = 2 ** (height - 2)
        everyone = gather_children(outgoing)
        arrived = block_of(everyone, position - gap, partitions, sep_rows) + block_of(
            everyone, position + gap, partitions, sep_rows
        )
        reduced, outgoing = settle(arrived, height, reduced, outgoing)
    everyone = gather_children(outgoing)
    reduced, outgoing = settle(
        block_of(everyone, partitions // 2, partitions, sep_rows), levels + 1, reduced, outgoing
    )
    top_value = jnp.einsum(
        "mij,cmi->cmj", separator_inverse, reduced, preferred_element_type=jnp.float32
    )
    solution = jnp.where(
        level_here == levels + 1, top_value, jnp.zeros(separator_source.shape, jnp.float32)
    )
    for height in range(levels, 0, -1):
        everyone = gather_parents(solution.astype(jnp.bfloat16))
        if height == levels:
            parent = position * 0
        else:
            parent = position // 2 ** (height + 1) * 2 ** (height + 1) + 2**height
        above = block_of(everyone, parent, partitions, sep_rows)
        residue = reduced.astype(jnp.float32) - jnp.einsum(
            "mij,cmi->cmj", upward_map, above, preferred_element_type=jnp.float32
        )
        fresh = jnp.einsum(
            "mij,cmi->cmj",
            separator_inverse,
            residue.astype(jnp.bfloat16),
            preferred_element_type=jnp.float32,
        )
        solution = jnp.where(level_here == height, fresh, solution)
    everyone = gather_parents(solution.astype(jnp.bfloat16))
    above = block_of(everyone, 2 * (position // 2) + 1, partitions, sep_rows)
    residue = leaf_solved.astype(jnp.float32) - jnp.einsum(
        "mij,cmi->cmj", leaf_map, above, preferred_element_type=jnp.float32
    )
    azimuthal_field = jnp.einsum(
        "mkji,cmkj->cmki",
        leaf_inverse,
        residue.astype(jnp.bfloat16).reshape(2, modes_dev, blocks_dev, block_width),
        preferred_element_type=jnp.float32,
    ).reshape(2, modes_dev, nodes_dev)
    return (nonlinear, azimuthal_field, solution)


def solution(mesh):
    in_specs = (
        P(None, None, "mode", "mesh"),
        P(None, None, "mode", "mesh"),
        P("mode", "mesh", None, None),
        P("mode", None, "mesh"),
        P("mode", "mesh", None),
        P("mode", "mesh", None),
        P(None, "mode", "mesh"),
        P("mesh", None, None),
    )
    out_specs = (P(None, None, "mode", "mesh"), P(None, "mode", "mesh"), P(None, "mode", "mesh"))
    return jax.shard_map(shards, mesh=mesh, in_specs=in_specs, out_specs=out_specs, check_vma=False)
```

profile of v0, /device:TPU:1, one launch (start us, length us, event | category | flops | bytes accessed | tf_op | source)
XLA Modules:
  0.0 287.9 jit_solution(11790060930523183828)
XLA Ops:
  10.9 24.6 %gather_fusion = bf16[128,16,2560]{2,0,1:T(8,128)(2,1)} fusion(bf16[16,128,2560]{2,1,0:T(8,128)(2,1)} %param.11, s32[1024]{0:T(1024)S(1)} %get-tuple-element.29), kind=kCustom, calls=%fused_computation | custom fusion | bytes 20972032 | tf_op jit(solution)/shard_map/jit(_take)/gather | solution.py:120
  36.1 24.0 %all-gather.2.cloned.1.call-done = bf16[6,2,64,2560]{3,2,1,0:T(8,128)(2,1)} async-done(((bf16[6,2,16,2560]{3,2,1,0:T(8,128)(2,1)}), bf16[6,2,64,2560]{3,2,1,0:T(8,128)(2,1)}) %all-gather.2.cloned.1.call-update) | async-done | bytes 3932176 | tf_op jit(solution)/shard_map/all_gather | solution.py:31
  67.3 8.1 %fusion.19 = bf16[2,16,2560]{2,0,1:T(2,128)(2,1)S(1)} fusion(bf16[16,20,128,128]{3,2,1,0:T(8,128)(2,1)} %param.10, bf16[2,16,20,128]{3,2,1,0:T(8,128)(2,1)S(1)} %convert_element_type.186), kind=kOutput, calls=%fused_computation.24 | convolution fusion | flops 21053440 | bytes 10813440 | tf_op jit(solution)/shard_map/mkij,cmkj->cmki/dot_general | solution.py:110
  75.4 5.7 %fusion.25 = f32[2,16,128]{2,0,1:T(2,128)S(1)} fusion(bf16[2,16,2560]{2,0,1:T(2,128)(2,1)S(1)} %fusion.19, bf16[128,16,2560]{2,0,1:T(8,128)(2,1)} %gather_fusion, pred[128]{0:T(512)(128)(4,1)S(1)} %get-tuple-element.19), kind=kOutput, calls=%fused_computation.26 | convolution fusion | flops 26214400 | bytes 10666112 | tf_op jit(solution)/shard_map/mij,cmj->cmi/dot_general | solution.py:122
  82.0 7.8 %all-to-all-start = ((f32[32,2,16,128]{3,2,1,0:T(8,128)}), f32[32,2,16,128]{3,2,1,0:T(8,128)S(1)}, u32[]{:S(2)}, u32[]{:S(2)}) async-start(f32[32,2,16,128]{3,2,1,0:T(8,128)} %broadcast_in_dim.58), calls=%async_computation | async-start | bytes 1048576 | tf_op jit(solution)/shard_map/all_to_all | solution.py:15
  92.7 8.7 %all-to-all-done = f32[32,2,16,128]{3,2,1,0:T(8,128)S(1)} async-done(((f32[32,2,16,128]{3,2,1,0:T(8,128)}), f32[32,2,16,128]{3,2,1,0:T(8,128)S(1)}, u32[]{:S(2)}, u32[]{:S(2)}) %all-to-all-start) | async-done | bytes 524320 | tf_op jit(solution)/shard_map/all_to_all | solution.py:15
  106.9 11.5 %all-to-all-done.1 = f32[32,2,16,128]{3,2,1,0:T(8,128)S(1)} async-done(((f32[32,2,16,128]{3,2,1,0:T(8,128)}), f32[32,2,16,128]{3,2,1,0:T(8,128)S(1)}, u32[]{:S(2)}, u32[]{:S(2)}) %all-to-all-start.1) | async-done | bytes 524320 | tf_op jit(solution)/shard_map/all_to_all | solution.py:15
  123.9 11.5 %all-to-all-done.2 = f32[32,2,16,128]{3,2,1,0:T(8,128)S(1)} async-done(((f32[32,2,16,128]{3,2,1,0:T(8,128)}), f32[32,2,16,128]{3,2,1,0:T(8,128)S(1)}, u32[]{:S(2)}, u32[]{:S(2)}) %all-to-all-start.2) | async-done | bytes 524320 | tf_op jit(solution)/shard_map/all_to_all | solution.py:15
  140.9 11.5 %all-to-all-done.3 = f32[32,2,16,128]{3,2,1,0:T(8,128)S(1)} async-done(((f32[32,2,16,128]{3,2,1,0:T(8,128)}), f32[32,2,16,128]{3,2,1,0:T(8,128)S(1)}, u32[]{:S(2)}, u32[]{:S(2)}) %all-to-all-start.3) | async-done | bytes 524320 | tf_op jit(solution)/shard_map/all_to_all | solution.py:15
  154.2 3.9 %all-to-all-start.4 = ((f32[32,2,16,128]{3,2,1,0:T(8,128)}), f32[32,2,16,128]{3,2,1,0:T(8,128)S(1)}, u32[]{:S(2)}, u32[]{:S(2)}) async-start(f32[32,2,16,128]{3,2,1,0:T(8,128)} %broadcast_in_dim.64), calls=%async_computation.4 | async-start | bytes 1048576 | tf_op jit(solution)/shard_map/all_to_all | solution.py:15
  158.1 11.3 %all-to-all-done.4 = f32[32,2,16,128]{3,2,1,0:T(8,128)S(1)} async-done(((f32[32,2,16,128]{3,2,1,0:T(8,128)}), f32[32,2,16,128]{3,2,1,0:T(8,128)S(1)}, u32[]{:S(2)}, u32[]{:S(2)}) %all-to-all-start.4) | async-done | bytes 524320 | tf_op jit(solution)/shard_map/all_to_all | solution.py:15
  174.9 11.5 %all-to-all-done.5 = f32[32,2,16,128]{3,2,1,0:T(8,128)S(1)} async-done(((f32[32,2,16,128]{3,2,1,0:T(8,128)}), f32[32,2,16,128]{3,2,1,0:T(8,128)S(1)}, u32[]{:S(2)}, u32[]{:S(2)}) %all-to-all-start.5) | async-done | bytes 524320 | tf_op jit(solution)/shard_map/all_to_all | solution.py:15
  187.2 12.4 %all_to_all.60 = bf16[32,2,16,128]{3,2,1,0:T(8,128)(2,1)S(1)} all-to-all(bf16[32,2,16,128]{3,2,1,0:T(8,128)(2,1)S(1)} %broadcast_in_dim.118), channel_id=1, replica_groups=mesh['mode'=4,'mesh'=32] {'mesh'}, dimensions={0} | all-to-all | bytes 524288 | tf_op jit(solution)/shard_map/all_to_all | solution.py:15
  201.0 3.7 %all-to-all-start.7 = ((bf16[32,2,16,128]{3,2,1,0:T(8,128)(2,1)}), bf16[32,2,16,128]{3,2,1,0:T(8,128)(2,1)S(1)}, u32[]{:S(2)}, u32[]{:S(2)}) async-start(bf16[32,2,16,128]{3,2,1,0:T(8,128)(2,1)} %broadcast_in_dim.119), calls=%async_computation.7 | async-start | bytes 524288 | tf_op jit(solution)/shard_map/all_to_all | solution.py:15
  204.7 9.0 %all-to-all-done.7 = bf16[32,2,16,128]{3,2,1,0:T(8,128)(2,1)S(1)} async-done(((bf16[32,2,16,128]{3,2,1,0:T(8,128)(2,1)}), bf16[32,2,16,128]{3,2,1,0:T(8,128)(2,1)S(1)}, u32[]{:S(2)}, u32[]{:S(2)}) %all-to-all-start.7) | async-done | bytes 262176 | tf_op jit(solution)/shard_map/all_to_all | solution.py:15
  215.1 3.7 %all-to-all-start.8 = ((bf16[32,2,16,128]{3,2,1,0:T(8,128)(2,1)}), bf16[32,2,16,128]{3,2,1,0:T(8,128)(2,1)S(1)}, u32[]{:S(2)}, u32[]{:S(2)}) async-start(bf16[32,2,16,128]{3,2,1,0:T(8,128)(2,1)} %broadcast_in_dim.120), calls=%async_computation.8 | async-start | bytes 524288 | tf_op jit(solution)/shard_map/all_to_all | solution.py:15
  218.9 9.1 %all-to-all-done.8 = bf16[32,2,16,128]{3,2,1,0:T(8,128)(2,1)S(1)} async-done(((bf16[32,2,16,128]{3,2,1,0:T(8,128)(2,1)}), bf16[32,2,16,128]{3,2,1,0:T(8,128)(2,1)S(1)}, u32[]{:S(2)}, u32[]{:S(2)}) %all-to-all-start.8) | async-done | bytes 262176 | tf_op jit(solution)/shard_map/all_to_all | solution.py:15
  229.3 3.7 %all-to-all-start.9 = ((bf16[32,2,16,128]{3,2,1,0:T(8,128)(2,1)}), bf16[32,2,16,128]{3,2,1,0:T(8,128)(2,1)S(1)}, u32[]{:S(2)}, u32[]{:S(2)}) async-start(bf16[32,2,16,128]{3,2,1,0:T(8,128)(2,1)} %broadcast_in_dim.121), calls=%async_computation.9 | async-start | bytes 524288 | tf_op jit(solution)/shard_map/all_to_all | solution.py:15
  233.1 9.1 %all-to-all-done.9 = bf16[32,2,16,128]{3,2,1,0:T(8,128)(2,1)S(1)} async-done(((bf16[32,2,16,128]{3,2,1,0:T(8,128)(2,1)}), bf16[32,2,16,128]{3,2,1,0:T(8,128)(2,1)S(1)}, u32[]{:S(2)}, u32[]{:S(2)}) %all-to-all-start.9) | async-done | bytes 262176 | tf_op jit(solution)/shard_map/all_to_all | solution.py:15
  243.5 3.7 %all-to-all-start.10 = ((bf16[32,2,16,128]{3,2,1,0:T(8,128)(2,1)}), bf16[32,2,16,128]{3,2,1,0:T(8,128)(2,1)S(1)}, u32[]{:S(2)}, u32[]{:S(2)}) async-start(bf16[32,2,16,128]{3,2,1,0:T(8,128)(2,1)} %broadcast_in_dim.122), calls=%async_computation.10 | async-start | bytes 524288 | tf_op jit(solution)/shard_map/all_to_all | solution.py:15
  247.3 9.1 %all-to-all-done.10 = bf16[32,2,16,128]{3,2,1,0:T(8,128)(2,1)S(1)} async-done(((bf16[32,2,16,128]{3,2,1,0:T(8,128)(2,1)}), bf16[32,2,16,128]{3,2,1,0:T(8,128)(2,1)S(1)}, u32[]{:S(2)}, u32[]{:S(2)}) %all-to-all-start.10) | async-done | bytes 262176 | tf_op jit(solution)/shard_map/all_to_all | solution.py:15
  257.8 3.7 %all-to-all-start.11 = ((bf16[32,2,16,128]{3,1,2,0:T(2,128)(2,1)}), bf16[32,2,16,128]{3,1,2,0:T(2,128)(2,1)S(1)}, u32[]{:S(2)}, u32[]{:S(2)}) async-start(bf16[32,2,16,128]{3,1,2,0:T(2,128)(2,1)} %broadcast_in_dim.123), calls=%async_computation.11 | async-start | bytes 524288 | tf_op jit(solution)/shard_map/all_to_all | solution.py:15
  262.1 8.4 %all-to-all-done.11 = bf16[32,2,16,128]{3,1,2,0:T(2,128)(2,1)S(1)} async-done(((bf16[32,2,16,128]{3,1,2,0:T(2,128)(2,1)}), bf16[32,2,16,128]{3,1,2,0:T(2,128)(2,1)S(1)}, u32[]{:S(2)}, u32[]{:S(2)}) %all-to-all-start.11) | async-done | bytes 262176 | tf_op jit(solution)/shard_map/all_to_all | solution.py:15
  270.8 9.4 %convolution_bitcast_fusion.2 = f32[2,16,20,128]{3,0,2,1:T(2,128)S(1)} fusion(bf16[16,20,128,128]{3,2,1,0:T(8,128)(2,1)} %param.10, bf16[128,16,2560]{2,0,1:T(8,128)(2,1)} %gather_fusion, pred[128]{0:T(512)(128)(4,1)S(1)} %get-tuple-element.19, bf16[2,16,2560]{2,0,1:T(2,128)(2,1)S(1)} %fusion.19, bf16[2,16,4096]{2,0,1:T(2,128)(2,1)S(1)} %copy_bitcast_fusion.6, ...), kind=kOutput, calls=%fused_computation.22 | convolution fusion | flops 47431680 | bytes 21471748 | tf_op jit(solution)/shard_map/mkji,cmkj->cmki/dot_general | solution.py:190
  (105 shorter events, 48.0 us)
Async XLA Ops:
  7.2 82.7 %copy-start = (bf16[16,128,128]{2,1,0:T(8,128)(2,1)S(1)}, bf16[16,128,128]{2,1,0:T(8,128)(2,1)}, u32[]{:S(2)}) copy-start(bf16[16,128,128]{2,1,0:T(8,128)(2,1)} %param.13) | copy-start | bytes 1572868
  7.2 3.7 %copy-start.5 = (s32[1,2,128]{2,1,0:T(2,128)S(1)}, s32[1,2,128]{2,1,0:T(2,128)}, u32[]{:S(2)}) copy-start(s32[1,2,128]{2,1,0:T(2,128)} %param.15) | copy-start | bytes 3076
  7.2 52.9 %all-gather.2.cloned.1.call-start = ((), (), s32[]{:S(2)}) async-start(), calls=%async_computation.12 | async-start | bytes 4915200 | tf_op jit(solution)/shard_map/all_gather | solution.py:31
  60.1 2.7 copy-start.2
  65.9 9.5 %copy-start.4 = (f32[3,2,16,2560]{3,2,1,0:T(8,128)}, f32[3,2,16,2560]{3,2,1,0:T(8,128)S(1)}, u32[]{:S(2)}) copy-start(f32[3,2,16,2560]{3,2,1,0:T(8,128)S(1)} %fusion.9) | copy-start | bytes 2949124
  81.1 20.4 %copy-start.3 = (f32[2,16,128]{2,1,0:T(8,128)S(1)}, f32[2,16,128]{2,1,0:T(8,128)}, u32[]{:S(2)}) copy-start(f32[2,16,128]{2,1,0:T(8,128)} %param.14) | copy-start | bytes 49156
  81.1 20.4 %copy-start.1 = (bf16[16,128,128]{2,1,0:T(8,128)(2,1)S(1)}, bf16[16,128,128]{2,1,0:T(8,128)(2,1)}, u32[]{:S(2)}) copy-start(bf16[16,128,128]{2,1,0:T(8,128)(2,1)} %param.12) | copy-start | bytes 1572868
  82.0 19.4 %all-to-all-start = ((f32[32,2,16,128]{3,2,1,0:T(8,128)}), f32[32,2,16,128]{3,2,1,0:T(8,128)S(1)}, u32[]{:S(2)}, u32[]{:S(2)}) async-start(f32[32,2,16,128]{3,2,1,0:T(8,128)} %broadcast_in_dim.58), calls=%async_computation | async-start | bytes 1048576 | tf_op jit(solution)/shard_map/all_to_all | solution.py:15
  103.2 15.2 %all-to-all-start.1 = ((f32[32,2,16,128]{3,2,1,0:T(8,128)}), f32[32,2,16,128]{3,2,1,0:T(8,128)S(1)}, u32[]{:S(2)}, u32[]{:S(2)}) async-start(f32[32,2,16,128]{3,2,1,0:T(8,128)} %broadcast_in_dim.61), calls=%async_computation.1 | async-start | bytes 1048576 | tf_op jit(solution)/shard_map/all_to_all | solution.py:15
  120.2 15.2 %all-to-all-start.2 = ((f32[32,2,16,128]{3,2,1,0:T(8,128)}), f32[32,2,16,128]{3,2,1,0:T(8,128)S(1)}, u32[]{:S(2)}, u32[]{:S(2)}) async-start(f32[32,2,16,128]{3,2,1,0:T(8,128)} %broadcast_in_dim.62), calls=%async_computation.2 | async-start | bytes 1048576 | tf_op jit(solution)/shard_map/all_to_all | solution.py:15
  137.2 15.2 %all-to-all-start.3 = ((f32[32,2,16,128]{3,2,1,0:T(8,128)}), f32[32,2,16,128]{3,2,1,0:T(8,128)S(1)}, u32[]{:S(2)}, u32[]{:S(2)}) async-start(f32[32,2,16,128]{3,2,1,0:T(8,128)} %broadcast_in_dim.63), calls=%async_computation.3 | async-start | bytes 1048576 | tf_op jit(solution)/shard_map/all_to_all | solution.py:15
  154.2 15.2 %all-to-all-start.4 = ((f32[32,2,16,128]{3,2,1,0:T(8,128)}), f32[32,2,16,128]{3,2,1,0:T(8,128)S(1)}, u32[]{:S(2)}, u32[]{:S(2)}) async-start(f32[32,2,16,128]{3,2,1,0:T(8,128)} %broadcast_in_dim.64), calls=%async_computation.4 | async-start | bytes 1048576 | tf_op jit(solution)/shard_map/all_to_all | solution.py:15
  171.2 15.2 %all-to-all-start.5 = ((f32[32,2,16,128]{3,2,1,0:T(8,128)}), f32[32,2,16,128]{3,2,1,0:T(8,128)S(1)}, u32[]{:S(2)}, u32[]{:S(2)}) async-start(f32[32,2,16,128]{3,2,1,0:T(8,128)} %broadcast_in_dim.65), calls=%async_computation.5 | async-start | bytes 1048576 | tf_op jit(solution)/shard_map/all_to_all | solution.py:15
  201.0 12.8 %all-to-all-start.7 = ((bf16[32,2,16,128]{3,2,1,0:T(8,128)(2,1)}), bf16[32,2,16,128]{3,2,1,0:T(8,128)(2,1)S(1)}, u32[]{:S(2)}, u32[]{:S(2)}) async-start(bf16[32,2,16,128]{3,2,1,0:T(8,128)(2,1)} %broadcast_in_dim.119), calls=%async_computation.7 | async-start | bytes 524288 | tf_op jit(solution)/shard_map/all_to_all | solution.py:15
  215.1 12.8 %all-to-all-start.8 = ((bf16[32,2,16,128]{3,2,1,0:T(8,128)(2,1)}), bf16[32,2,16,128]{3,2,1,0:T(8,128)(2,1)S(1)}, u32[]{:S(2)}, u32[]{:S(2)}) async-start(bf16[32,2,16,128]{3,2,1,0:T(8,128)(2,1)} %broadcast_in_dim.120), calls=%async_computation.8 | async-start | bytes 524288 | tf_op jit(solution)/shard_map/all_to_all | solution.py:15
  229.3 12.8 %all-to-all-start.9 = ((bf16[32,2,16,128]{3,2,1,0:T(8,128)(2,1)}), bf16[32,2,16,128]{3,2,1,0:T(8,128)(2,1)S(1)}, u32[]{:S(2)}, u32[]{:S(2)}) async-start(bf16[32,2,16,128]{3,2,1,0:T(8,128)(2,1)} %broadcast_in_dim.121), calls=%async_computation.9 | async-start | bytes 524288 | tf_op jit(solution)/shard_map/all_to_all | solution.py:15
  243.5 12.8 %all-to-all-start.10 = ((bf16[32,2,16,128]{3,2,1,0:T(8,128)(2,1)}), bf16[32,2,16,128]{3,2,1,0:T(8,128)(2,1)S(1)}, u32[]{:S(2)}, u32[]{:S(2)}) async-start(bf16[32,2,16,128]{3,2,1,0:T(8,128)(2,1)} %broadcast_in_dim.122), calls=%async_computation.10 | async-start | bytes 524288 | tf_op jit(solution)/shard_map/all_to_all | solution.py:15
  257.8 12.8 %all-to-all-start.11 = ((bf16[32,2,16,128]{3,1,2,0:T(2,128)(2,1)}), bf16[32,2,16,128]{3,1,2,0:T(2,128)(2,1)S(1)}, u32[]{:S(2)}, u32[]{:S(2)}) async-start(bf16[32,2,16,128]{3,1,2,0:T(2,128)(2,1)} %broadcast_in_dim.123), calls=%async_computation.11 | async-start | bytes 524288 | tf_op jit(solution)/shard_map/all_to_all | solution.py:15
Sparse Core Ops, SparseCore 0:
  11.0 49.0 all-gather.1
where the time goes:
time: 289 us; the launch traced here: 288 us
  waiting for transfers between devices  135 us (47%)
  starting transfers between devices  45 us (16%)
  local copies, waits for them, and re-layouts  39.5 us (14%)
  matrix products  34.4 us (12%)
  between operations  14.7 us (5%)
  blocking collectives  12.4 us (4%)
  other arithmetic  7.11 us (2%)
    all_to_all x11, waiting for transfers between devices, sent_to_all(): lax.all_to_all(jnp.broadcast_to(x[None], (length, *x.shape)), axis, 0, 0,...  111 us
    all_to_all x11, starting transfers between devices, sent_to_all(): lax.all_to_all(jnp.broadcast_to(x[None], (length, *x.shape)), axis, 0, 0,...  45 us
    gather x1, local copies, waits for them, and re-layouts, shards(): leaf_map = jnp.take(leaf_coupling, row_order[0], axis=1)  24.6 us
    all_gather x1, waiting for transfers between devices, in_one_piece(): lax.all_gather(both, axis, axis=dim, tiled=True)  24 us
    all_to_all x1, blocking collectives, sent_to_all(): lax.all_to_all(jnp.broadcast_to(x[None], (length, *x.shape)), axis, 0, 0,...  12.4 us
    dot_general x1, matrix products, shards(): jnp.einsum('mkji,cmkj->cmki', leaf_inverse, residue.astype(jnp.bfloat16)....  9.37 us
    broadcast_in_dim x12, local copies, waits for them, and re-layouts, sent_to_all(): jnp.broadcast_to(x[None], (length, *x.shape))  9.12 us
    dot_general x1, matrix products, shards(): jnp.einsum('mkij,cmkj->cmki', leaf_inverse, source.reshape(2, modes_dev,...  8.09 us
  transfers between devices with their start and end apart: 12, of which 12 were waited for; matrix products, arithmetic and copies ran while one was open for 10% of the time, Pallas kernels for 0%

commit v1 on v0

v1 whole, which is shorter than its diff:
```python
import jax
import jax.numpy as jnp
import numpy as np
from jax import lax
from jax.experimental import pallas as pl
from jax.experimental.pallas import tpu as pltpu
from jax.sharding import PartitionSpec as P

M = 64
NPHI = 192
DT = 0.5
MESH = pl.DeviceIdType.MESH
F32 = jnp.float32
BF16 = jnp.bfloat16

SLOT_OF = ((0, 0), (0, 2), (1, 0), (1, 2), (0, 1), (1, 1))
VR, VZ, BR, BZ, VP, BP = range(6)


def tables(parts):
    local = M // parts
    k = np.arange(NPHI)[:, None]
    m = np.arange(M)[None, :]
    phase = ((k * m) % NPHI) * (2.0 * np.pi / NPHI)
    both = np.stack([np.cos(phase), np.sin(phase)])
    both = both.reshape(2, NPHI, parts, local).transpose(1, 2, 0, 3).reshape(NPHI, 2 * M)
    weights = np.where(np.arange(M) == 0, 1.0, 2.0) / NPHI
    w = np.broadcast_to(weights.reshape(parts, 1, local), (parts, 2, local)).reshape(2 * M)
    return jnp.asarray(both, BF16), jnp.asarray((both * w).T, BF16)


def dot(a, b):
    return jnp.dot(a, b, preferred_element_type=F32)


def dot_nt(a, b):
    return lax.dot_general(a, b, (((1,), (1,)), ((), ())), preferred_element_type=F32)


def level_of(q, levels):
    return levels + 1 if q == 0 else (q & -q).bit_length()


def parent_of(q, levels):
    level = level_of(q, levels)
    if level == levels:
        return 0
    return (q >> (level + 1) << (level + 1)) + 2**level


def kernel(
    parts, places,
    vel, mag, linv, lcpl, sinv, scpl, ssrc, rows, tab_f, tab_b,
    nl_out, az_out, sol_out,
    stage, vb, xr, tf, tb, nb, nr, nl32, src16, lin, gup, smat, cmat, hmat, ssv, rowv, pt0, p1,
    srcb, ubuf, urow, hs, ss, srcs, us, xo, xin, ls, az, sol,
    sem_vb, sem_tab, sem_small, sem_lin, sem_g, sem_s1, sem_r1, sem_own, sem_s2, sem_r2, sem_own2,
    sem_ss, sem_sh, sem_sc, sem_rs, sem_rh, sem_rc, sem_us, sem_ur, sem_xs, sem_xr, sem_out,
):
    modes = src16.shape[0] // 2
    nodes = src16.shape[1]
    chunk = nodes // parts
    blocks = lin.shape[1]
    levels = places.bit_length() - 1
    y = lax.axis_index("mode")
    me = lax.axis_index("mesh")
    solver = lax.rem(me, 2) == 1

    def lanes_of(part):
        return pl.ds(pl.multiple_of(part * chunk, 128), chunk)

    def drain(ref, sem):
        pltpu.make_async_copy(ref, ref, sem).wait()

    for slot, (which, comp) in enumerate(SLOT_OF):
        pltpu.make_async_copy((vel, mag)[which].at[comp], stage.at[slot], sem_vb.at[slot]).start()
    small = ((sinv, smat), (scpl, cmat), (ssrc, ssv), (rows, rowv), (tab_f, tf), (tab_b, tb))
    for i, (a, b) in enumerate(small):
        pltpu.make_async_copy(a, b, sem_small.at[i]).start()

    def load_mode(m, carry):
        pltpu.make_async_copy(linv.at[m], lin.at[m], sem_lin.at[m]).start()
        pltpu.make_async_copy(lcpl.at[m], gup.at[m], sem_g.at[m]).start()
        return carry

    lax.fori_loop(0, modes, load_mode, 0)

    barrier = pltpu.get_barrier_semaphore()

    def greet(i, carry):
        other = lax.rem(me + i, places)
        pl.semaphore_signal(barrier, inc=1, device_id=(y, other), device_id_type=MESH)
        return carry

    for d in range(1, parts):
        pl.semaphore_signal(barrier, inc=1, device_id=(lax.rem(y + d, parts), me), device_id_type=MESH)
    lax.fori_loop(1, places, greet, 0)

    for slot in range(4):
        drain(stage.at[slot], sem_vb.at[slot])
        vb[slot] = stage[slot].astype(BF16)
    pl.semaphore_wait(barrier, parts - 1 + places - 1)

    def exchange(group, lo, hi):
        for d in range(1, parts):
            other = lax.rem(y + d, parts)
            pltpu.make_async_remote_copy(
                src_ref=vb.at[lo:hi, :, :, lanes_of(other)], dst_ref=xr.at[lo:hi, y],
                send_sem=sem_s1.at[group, d - 1], recv_sem=sem_r1.at[group, d - 1],
                device_id=(other, me), device_id_type=MESH,
            ).start()
        pltpu.make_async_copy(vb.at[lo:hi, :, :, lanes_of(y)], xr.at[lo:hi, y], sem_own.at[group]).start()

    def exchanged(group, lo, hi):
        for d in range(1, parts):
            drain(xr.at[lo:hi, 0], sem_r1.at[group, d - 1])
        drain(xr.at[lo:hi, 0], sem_own.at[group])

    exchange(0, 0, 4)
    for slot in range(4, 6):
        drain(stage.at[slot], sem_vb.at[slot])
        vb[slot] = stage[slot].astype(BF16)

    for i, (a, b) in enumerate(small):
        drain(b, sem_small.at[i])

    def for_solvers(act, own):
        def one(m, carry):
            there = 2 * m + 1
            pl.when(there != me)(lambda: act(m, there))
            pl.when(there == me)(lambda: own(m))
            return carry

        lax.fori_loop(0, modes, one, 0)

    def remote(src, dst, send, recv, there):
        return pltpu.make_async_remote_copy(
            src_ref=src, dst_ref=dst, send_sem=send, recv_sem=recv, device_id=(y, there), device_id_type=MESH
        )

    srow = lax.broadcasted_iota(jnp.int32, (128, 128), 0)
    pt0[...] = (srow == jnp.broadcast_to(rowv[0, 0:1, :], (128, 128))).astype(F32).astype(BF16)
    p1[...] = (srow == jnp.broadcast_to(rowv[0, 1:2, :], (128, 128))).astype(F32).T.astype(BF16)

    def build_h(m, carry):
        coupling = dot(p1[...], cmat[m]).astype(BF16)
        hmat[m] = dot(coupling, smat[m]).astype(BF16)
        return carry

    lax.fori_loop(0, modes, build_h, 0, unroll=4)
    srcb[...] = jnp.zeros_like(srcb)
    ubuf[...] = jnp.zeros_like(ubuf)
    for m in range(modes):
        for c in range(2):
            srcb[m, c : c + 1, :] = ssv[c, m : m + 1, :]
    for_solvers(
        lambda m, t: remote(hmat.at[m], hs.at[me], sem_sh.at[m], sem_rh, t).start(),
        lambda m: pltpu.make_async_copy(hmat.at[m], hs.at[me], sem_rh).start(),
    )
    for_solvers(
        lambda m, t: remote(srcb.at[m], srcs.at[me], sem_sc.at[m], sem_rc, t).start(),
        lambda m: pltpu.make_async_copy(srcb.at[m], srcs.at[me], sem_rc).start(),
    )
    for_solvers(
        lambda m, t: remote(smat.at[m], ss.at[me], sem_ss.at[m], sem_rs, t).start(),
        lambda m: pltpu.make_async_copy(smat.at[m], ss.at[me], sem_rs).start(),
    )

    def build_g(m, carry):
        drain(lin.at[m], sem_lin.at[m])
        drain(gup.at[m], sem_g.at[m])
        for b in range(blocks):
            at = slice(b * 128, (b + 1) * 128)
            gup[m, :, at] = dot(gup[m, :, at], lin[m, b]).astype(BF16)
        return carry

    lax.fori_loop(0, modes, build_g, 0)

    def transform(jobs):
        at = 0
        while at < chunk:
            width = min(256, chunk - at)
            here = slice(at, at + width)
            need = sorted({s for _, pairs in jobs for s in pairs})
            phys = {s: dot(tf[...], xr[s, :, :, :, here].reshape(2 * M, width)) for s in need}
            for comp, (a, b, c, d) in jobs:
                crossed = phys[a] * phys[b] - phys[c] * phys[d]
                back = dot(tb[...], crossed.astype(BF16)).astype(BF16)
                nb[comp, :, :, :, here] = back.reshape(parts, 2, modes, width)
            at += width

    def give_back(group, comp):
        for d in range(1, parts):
            other = lax.rem(y + d, parts)
            pltpu.make_async_remote_copy(
                src_ref=nb.at[comp, other], dst_ref=nr.at[comp, :, :, lanes_of(y)],
                send_sem=sem_s2.at[group, d - 1], recv_sem=sem_r2.at[group, d - 1],
                device_id=(other, me), device_id_type=MESH,
            ).start()
        pltpu.make_async_copy(nb.at[comp, y], nr.at[comp, :, :, lanes_of(y)], sem_own2.at[group]).start()

    def given_back(group, comp):
        for d in range(1, parts):
            drain(nb.at[comp, 0], sem_r2.at[group, d - 1])
        drain(nb.at[comp, 0], sem_own2.at[group])

    exchanged(0, 0, 4)
    transform([(1, (VZ, BR, VR, BZ))])
    give_back(0, 1)
    exchange(1, 4, 6)

    given_back(0, 1)
    phi = nr[1].astype(F32)
    nl32[1] = phi
    source = stage[BP] + DT * phi
    src16[...] = source.astype(BF16).reshape(2 * modes, nodes)
    pltpu.make_async_copy(nl32.at[1], nl_out.at[1], sem_out.at[0]).start()

    mode_of = lax.rem(lax.broadcasted_iota(jnp.int32, (2 * modes, 128), 0), modes)

    def update(m, acc):
        return jnp.where(mode_of == m, dot_nt(src16[...], gup[m]), acc)

    leaf_update = lax.fori_loop(0, modes, update, jnp.zeros((2 * modes, 128), F32), unroll=4)
    urow[...] = dot(leaf_update.astype(BF16), pt0[...])
    for m in range(modes):
        for c in range(2):
            ubuf[m, c : c + 1, :] = urow[c * modes + m : c * modes + m + 1, :]
    for_solvers(
        lambda m, t: remote(ubuf.at[m], us.at[me], sem_us.at[m], sem_ur, t).start(),
        lambda m: pltpu.make_async_copy(ubuf.at[m], us.at[me], sem_ur).start(),
    )

    exchanged(1, 4, 6)
    transform([(0, (VP, BZ, VZ, BP)), (2, (VR, BP, VP, BR))])
    give_back(1, 0)
    give_back(2, 2)

    def leaf_forward(m, carry):
        for b in range(blocks):
            at = slice(b * 128, (b + 1) * 128)
            ls[:, at] = jnp.where(mode_of == m, dot_nt(src16[:, at], lin[m, b]), ls[:, at])
        return carry

    ls[...] = jnp.zeros_like(ls)
    lax.fori_loop(0, modes, leaf_forward, 0)

    @pl.when(solver)
    def _():
        drain(hs, sem_rh)
        drain(srcs, sem_rc)
        drain(us, sem_ur)
        drain(ss, sem_rs)
        out, w = {}, {}
        order = sorted(range(places), key=lambda q: level_of(q, levels))
        for q in order:
            level = level_of(q, levels)
            if level == 1:
                arrived = us[q - 1] + us[q]
            elif level <= levels:
                gap = 2 ** (level - 2)
                arrived = out[q - gap] + out[q + gap]
            else:
                arrived = out[places // 2]
            g = (srcs[q] - arrived).astype(BF16)
            if level <= levels:
                out[q] = dot_nt(g, hs[q])
            reduced = dot_nt(g, ss[q]).astype(BF16)
            w[q] = dot(reduced, ss[q])
        x = {0: w[0]}
        for q in order[::-1][1:]:
            x[q] = w[q] - dot(x[parent_of(q, levels)].astype(BF16), hs[q])
        first = lax.broadcasted_iota(jnp.int32, (8, 128), 0) < 2
        for p in range(places):
            xo[p] = jnp.where(first, x[p], pltpu.roll(x[2 * (p // 2) + 1], 2, 0))

        def send(p, carry):
            def away():
                pltpu.make_async_remote_copy(
                    src_ref=xo.at[p], dst_ref=xin.at[lax.div(me, 2)], send_sem=sem_xs.at[p], recv_sem=sem_xr,
                    device_id=(y, p), device_id_type=MESH,
                ).start()

            pl.when(p != me)(away)
            pl.when(p == me)(lambda: pltpu.make_async_copy(xo.at[p], xin.at[lax.div(me, 2)], sem_xr).start())
            return carry

        lax.fori_loop(0, places, send, 0)

    def leaf_back(b, carry):
        at = pl.ds(pl.multiple_of(b * 128, 128), 128)
        own = ls[:, at].astype(BF16)
        acc = jnp.zeros((2 * modes, 128), F32)
        for m in range(modes):
            acc = jnp.where(mode_of == m, dot(own, lin[m, b]), acc)
        az[:, at] = acc
        return carry

    lax.fori_loop(0, blocks, leaf_back, 0)

    given_back(1, 0)
    given_back(2, 2)
    nl32[0] = nr[0].astype(F32)
    nl32[2] = nr[2].astype(F32)
    pltpu.make_async_copy(nl32.at[0], nl_out.at[0], sem_out.at[1]).start()
    pltpu.make_async_copy(nl32.at[2], nl_out.at[2], sem_out.at[2]).start()

    drain(xin, sem_xr)
    for m in range(modes):
        for c in range(2):
            sol[c, m : m + 1, :] = xin[m, c : c + 1, :]
            urow[c * modes + m : c * modes + m + 1, :] = xin[m, 2 + c : 3 + c, :]
    pltpu.make_async_copy(sol, sol_out, sem_out.at[3]).start()
    above = dot_nt(urow[...].astype(BF16), pt0[...]).astype(BF16)

    def finish(m, carry):
        mine = jnp.where(mode_of == m, above, jnp.zeros_like(above))
        az[...] -= dot(mine, gup[m])
        return carry

    lax.fori_loop(0, modes, finish, 0, unroll=2)
    pltpu.make_async_copy(az, az_out, sem_out.at[4]).start()

    for group, (lo, hi) in enumerate(((0, 4), (4, 6))):
        for d in range(1, parts):
            drain(xr.at[lo:hi, 0], sem_s1.at[group, d - 1])
    for group in range(3):
        for d in range(1, parts):
            drain(nb.at[0, 0], sem_s2.at[group, d - 1])

    def sent(m, carry):
        @pl.when(2 * m + 1 != me)
        def _():
            drain(hmat.at[m], sem_sh.at[m])
            drain(smat.at[m], sem_ss.at[m])
            drain(srcb.at[m], sem_sc.at[m])
            drain(ubuf.at[m], sem_us.at[m])

        return carry

    lax.fori_loop(0, modes, sent, 0)

    @pl.when(solver)
    def _():
        def one(p, carry):
            pl.when(p != me)(lambda: drain(xo.at[p], sem_xs.at[p]))
            return carry

        lax.fori_loop(0, places, one, 0)

    for i, ref in enumerate((nl32.at[1], nl32.at[0], nl32.at[2], sol, az)):
        drain(ref, sem_out.at[i])


def solution(mesh):
    parts, places = mesh.shape["mode"], mesh.shape["mesh"]
    in_specs = (
        P(None, None, "mode", "mesh"),
        P(None, None, "mode", "mesh"),
        P("mode", "mesh", None, None),
        P("mode", None, "mesh"),
        P("mode", "mesh", None),
        P("mode", "mesh", None),
        P(None, "mode", "mesh"),
        P("mesh", None, None),
    )
    out_specs = (P(None, None, "mode", "mesh"), P(None, "mode", "mesh"), P(None, "mode", "mesh"))

    def shards(vel, mag, linv, lcpl, sinv, scpl, ssrc, rows):
        modes, nodes = vel.shape[2], vel.shape[3]
        blocks = linv.shape[1]
        chunk = nodes // parts
        tab_f, tab_b = tables(parts)
        vm = pltpu.VMEM
        dma = pltpu.SemaphoreType.DMA
        scratch = [
            vm((6, 2, modes, nodes), F32),
            vm((6, 2, modes, nodes), BF16),
            vm((6, parts, 2, modes, chunk), BF16),
            vm((NPHI, 2 * M), BF16),
            vm((2 * M, NPHI), BF16),
            vm((3, parts, 2, modes, chunk), BF16),
            vm((3, 2, modes, nodes), BF16),
            vm((3, 2, modes, nodes), F32),
            vm((2 * modes, nodes), BF16),
            vm((modes, blocks, 128, 128), BF16),
            vm((modes, 128, nodes), BF16),
            vm((modes, 128, 128), BF16),
            vm((modes, 128, 128), BF16),
            vm((modes, 128, 128), BF16),
            vm((2, modes, 128), F32),
            vm((1, 2, 128), jnp.int32),
            vm((128, 128), BF16),
            vm((128, 128), BF16),
            vm((modes, 8, 128), F32),
            vm((modes, 8, 128), F32),
            vm((2 * modes, 128), F32),
            vm((places, 128, 128), BF16),
            vm((places, 128, 128), BF16),
            vm((places, 8, 128), F32),
            vm((places, 8, 128), F32),
            vm((places, 8, 128), F32),
            vm((modes, 8, 128), F32),
            vm((2 * modes, nodes), F32),
            vm((2 * modes, nodes), F32),
            vm((2, modes, 128), F32),
            dma((6,)), dma((1,)), dma((6,)), dma((modes,)), dma((modes,)),
            dma((2, parts - 1)), dma((2, parts - 1)), dma((2,)),
            dma((3, parts - 1)), dma((3, parts - 1)), dma((3,)),
            dma((modes,)), dma((modes,)), dma((modes,)), dma, dma, dma,
            dma((modes,)), dma, dma((places,)), dma, dma((5,)),
        ]
        any_spec = pl.BlockSpec(memory_space=pl.ANY)

        def body(*refs):
            kernel(parts, places, *refs)

        nl, az, sol = pl.pallas_call(
            body,
            name="dynamo",
            out_shape=(
                jax.ShapeDtypeStruct((3, 2, modes, nodes), F32),
                jax.ShapeDtypeStruct((2 * modes, nodes), F32),
                jax.ShapeDtypeStruct((2, modes, 128), F32),
            ),
            in_specs=[any_spec] * 10,
            out_specs=(any_spec,) * 3,
            scratch_shapes=scratch,
            compiler_params=pltpu.CompilerParams(
                collective_id=0, has_side_effects=True, vmem_limit_bytes=60 * 2**20
            ),
        )(vel, mag, linv, lcpl, sinv, scpl, ssrc, rows, tab_f, tab_b)
        return nl, az.reshape(2, modes, nodes), sol

    return jax.shard_map(shards, mesh=mesh, in_specs=in_specs, out_specs=out_specs, check_vma=False)
```

time: 289 us -> 56.3 us (0.19)
  waiting for transfers between devices: 135 us -> 0 us
  Pallas kernels: 0 us -> 50.1 us
  starting transfers between devices: 45 us -> 0 us
  matrix products: 34.4 us -> 0 us
  local copies, waits for them, and re-layouts: 39.5 us -> 5.25 us
  between operations: 14.7 us -> 0.64 us
  blocking collectives: 12.4 us -> 0 us
  other arithmetic: 7.11 us -> 0 us
    all_to_all x11 -> x0, waiting for transfers between devices: 111 us -> none  [sent_to_all(): lax.all_to_all(jnp.broadcast_to(x[None], (length, *x.shape)), axis, 0, 0,...]
    pallas_call x0 -> x1, Pallas kernels: none -> 50.1 us  [shards(): pl.pallas_call(body, name='dynamo', out_shape=(jax.ShapeDtypeStruct((3, 2...]
    all_to_all x11 -> x0, starting transfers between devices: 45 us -> none  [sent_to_all(): lax.all_to_all(jnp.broadcast_to(x[None], (length, *x.shape)), axis, 0, 0,...]
    dot_general x23 -> x0, matrix products: 34.4 us -> none  [the longest x1 9.37 us: shards(): jnp.einsum('mkji,cmkj->cmki', leaf_inverse, residue.astype(jnp.bfloat16)....]
    gather x2 -> x0, local copies, waits for them, and re-layouts: 27.4 us -> none  [the longest x1 24.6 us: shards(): leaf_map = jnp.take(leaf_coupling, row_order[0], axis=1)]
    all_gather x1 -> x0, waiting for transfers between devices: 24 us -> none  [in_one_piece(): lax.all_gather(both, axis, axis=dim, tiled=True)]
    all_to_all x1 -> x0, blocking collectives: 12.4 us -> none  [sent_to_all(): lax.all_to_all(jnp.broadcast_to(x[None], (length, *x.shape)), axis, 0, 0,...]
    broadcast_in_dim x12 -> x0, local copies, waits for them, and re-layouts: 9.12 us -> none  [sent_to_all(): jnp.broadcast_to(x[None], (length, *x.shape))]
  transfers between devices with their start and end apart: 12 -> 0, of which waited for: 12 -> 0; matrix products, arithmetic and copies ran while one was open for 10% -> 0% of each run, Pallas kernels for 0% -> 0%
where the time goes in v1:
time: 56.3 us; the launch traced here: 56 us
  Pallas kernels  50.1 us (89%)
  local copies, waits for them, and re-layouts  5.25 us (9%)
  between operations  0.64 us (1%)
    pallas_call x1, Pallas kernels, shards(): pl.pallas_call(body, name='dynamo', out_shape=(jax.ShapeDtypeStruct((3, 2...  50.1 us
    unnamed x3, local copies, waits for them, and re-layouts  5.25 us

profile of v1, /device:TPU:1, one launch (start us, length us, event | category | flops | bytes accessed | tf_op | source)
XLA Modules:
  0.0 56.0 jit_solution(1958954354380711270)
XLA Ops:
  0.6 50.1 %dynamo.1 = (f32[3,2,16,2560]{3,2,1,0:T(8,128)}, f32[32,2560]{1,0:T(8,128)}, f32[2,16,128]{2,1,0:T(8,128)}) custom-call(f32[3,2,16,2560]{3,2,1,0:T(8,128)} %refs_0_.1, f32[3,2,16,2560]{3,2,1,0:T(8,128)} %refs_1_.1, bf16[16,20,128,128]{3,2,1,0:T(8,128)(2,1)} %refs_2_.1, bf16[16,128,2560]{2,1,0:T(8,128)(2,1)} %refs_3_.1, bf16[16,128,128]{2,1,0:T(8,128)(2,1)} %refs_4_.1, ...), custom_call_target="tpu_custom_call" | custom-call | tf_op jit(solution)/shard_map/dynamo/pallas_call | solution.py:418
  50.8 2.2 %copy.16 = f32[3,2,16,2560]{3,2,1,0:T(8,128)} copy(f32[3,2,16,2560]{3,2,1,0:T(8,128)} %get-tuple-element.12) | data formatting | bytes 1966080
  53.0 1.7 %copy.17 = f32[2,16,2560]{2,1,0:T(8,128)} copy(f32[2,16,2560]{2,1,0:T(8,128)} %bitcast.1) | data formatting | bytes 655360
  54.7 1.3 %copy.18 = f32[2,16,128]{2,1,0:T(8,128)} copy(f32[2,16,128]{2,1,0:T(8,128)} %get-tuple-element.14) | data formatting | bytes 32768

commit v2 on v1

v2 whole, which is shorter than its diff:
```python
import jax
import jax.numpy as jnp
import numpy as np
from jax import lax
from jax.experimental import pallas as pl
from jax.experimental.pallas import tpu as pltpu
from jax.sharding import PartitionSpec as P

M = 64
NPHI = 192
DT = 0.5
MESH = pl.DeviceIdType.MESH
F32 = jnp.float32
BF16 = jnp.bfloat16

SLOT_OF = ((0, 0), (0, 2), (1, 0), (1, 2), (0, 1), (1, 1))
VR, VZ, BR, BZ, VP, BP = range(6)


def tables(parts):
    local = M // parts
    k = np.arange(NPHI)[:, None]
    m = np.arange(M)[None, :]
    phase = ((k * m) % NPHI) * (2.0 * np.pi / NPHI)
    both = np.stack([np.cos(phase), np.sin(phase)])
    both = both.reshape(2, NPHI, parts, local).transpose(1, 2, 0, 3).reshape(NPHI, 2 * M)
    weights = np.where(np.arange(M) == 0, 1.0, 2.0) / NPHI
    w = np.broadcast_to(weights.reshape(parts, 1, local), (parts, 2, local)).reshape(2 * M)
    return jnp.asarray(both, BF16), jnp.asarray((both * w).T, BF16)


def dot(a, b):
    return jnp.dot(a, b, preferred_element_type=F32)


def dot_nt(a, b):
    return lax.dot_general(a, b, (((1,), (1,)), ((), ())), preferred_element_type=F32)


def level_of(q, levels):
    return levels + 1 if q == 0 else (q & -q).bit_length()


def parent_of(q, levels):
    level = level_of(q, levels)
    if level == levels:
        return 0
    return (q >> (level + 1) << (level + 1)) + 2**level


def kernel(
    parts, places,
    vel, mag, linv, lcpl, sinv, scpl, ssrc, rows, tab_f, tab_b,
    nl32, az, sol,
    stage, vb, xr, tf, tb, nb, nr, src16, lin, gup, smat, cmat, hmat, ssv, rowv, pt0, p1,
    srcb, ubuf, urow, hs, ss, srcs, us, xo, xin, ls,
    sem_vb, sem_small, sem_lin, sem_g, sem_s1, sem_r1, sem_s2, sem_r2,
    sem_ss, sem_sh, sem_sc, sem_rs, sem_rh, sem_rc, sem_us, sem_ur, sem_xs, sem_xr,
):
    modes = src16.shape[0] // 2
    nodes = src16.shape[1]
    chunk = nodes // parts
    blocks = lin.shape[1]
    levels = places.bit_length() - 1
    y = lax.axis_index("mode")
    me = lax.axis_index("mesh")
    solver = lax.rem(me, 2) == 1

    def lanes_of(part):
        return pl.ds(pl.multiple_of(part * chunk, 128), chunk)

    def drain(ref, sem):
        pltpu.make_async_copy(ref, ref, sem).wait()

    for slot, (which, comp) in enumerate(SLOT_OF):
        pltpu.make_async_copy((vel, mag)[which].at[comp], stage.at[slot], sem_vb.at[slot]).start()
    barrier = pltpu.get_barrier_semaphore()

    def greet(i, carry):
        other = jnp.where(me + i >= places, me + i - places, me + i)
        pl.semaphore_signal(barrier, inc=1, device_id=(y, other), device_id_type=MESH)
        return carry

    for d in range(1, parts):
        pl.semaphore_signal(barrier, inc=1, device_id=(lax.rem(y + d, parts), me), device_id_type=MESH)
    lax.fori_loop(1, places, greet, 0)

    small = ((sinv, smat), (scpl, cmat), (ssrc, ssv), (rows, rowv), (tab_f, tf), (tab_b, tb))
    for i, (a, b) in enumerate(small):
        pltpu.make_async_copy(a, b, sem_small.at[i]).start()

    for slot in range(4):
        drain(stage.at[slot], sem_vb.at[slot])
        vb[slot] = stage[slot].astype(BF16)
    pl.semaphore_wait(barrier, parts - 1 + places - 1)

    def to_mode(src, dst, send, recv, other):
        return pltpu.make_async_remote_copy(
            src_ref=src, dst_ref=dst, send_sem=send, recv_sem=recv, device_id=(other, me), device_id_type=MESH
        )

    after, before = lax.rem(y + 1, parts), lax.rem(y + parts - 1, parts)

    def exchange(group, lo, hi):
        for d in (2, 3, 1):
            other = lax.rem(y + d, parts)
            to_mode(
                vb.at[lo:hi, :, :, lanes_of(other)], xr.at[lo:hi, y],
                sem_s1.at[group, d - 1], sem_r1.at[group, d - 1], other,
            ).start()
        for slot in range(lo, hi):
            xr[slot, y] = vb[slot, :, :, lanes_of(y)]

    def exchanged(group, lo, hi):
        for d in range(1, parts):
            drain(xr.at[lo:hi, 0], sem_r1.at[group, d - 1])

    exchange(0, 0, 4)
    def load_mode(m, carry):
        pltpu.make_async_copy(linv.at[m], lin.at[m], sem_lin.at[m]).start()
        pltpu.make_async_copy(lcpl.at[m], gup.at[m], sem_g.at[m]).start()
        return carry

    lax.fori_loop(0, modes, load_mode, 0)

    for slot in range(4, 6):
        drain(stage.at[slot], sem_vb.at[slot])
        vb[slot] = stage[slot].astype(BF16)

    for i, (a, b) in enumerate(small):
        drain(b, sem_small.at[i])

    def for_solvers(act, own):
        def one(m, carry):
            there = 2 * m + 1
            pl.when(there != me)(lambda: act(m, there))
            pl.when(there == me)(lambda: own(m))
            return carry

        lax.fori_loop(0, modes, one, 0)

    def remote(src, dst, send, recv, there):
        return pltpu.make_async_remote_copy(
            src_ref=src, dst_ref=dst, send_sem=send, recv_sem=recv, device_id=(y, there), device_id_type=MESH
        )

    for_solvers(
        lambda m, t: remote(smat.at[m], ss.at[me], sem_ss, sem_rs, t).start(),
        lambda m: pltpu.make_async_copy(smat.at[m], ss.at[me], sem_rs).start(),
    )
    srow = lax.broadcasted_iota(jnp.int32, (128, 128), 0)
    pt0[...] = (srow == jnp.broadcast_to(rowv[0, 0:1, :], (128, 128))).astype(F32).astype(BF16)
    p1[...] = (srow == jnp.broadcast_to(rowv[0, 1:2, :], (128, 128))).astype(F32).T.astype(BF16)

    def build_h(m, carry):
        coupling = dot(p1[...], cmat[m]).astype(BF16)
        hmat[m] = dot(coupling, smat[m]).astype(BF16)
        return carry

    lax.fori_loop(0, modes, build_h, 0, unroll=4)
    srcb[...] = jnp.zeros_like(srcb)
    ubuf[...] = jnp.zeros_like(ubuf)
    for m in range(modes):
        for c in range(2):
            srcb[m, c : c + 1, :] = ssv[c, m : m + 1, :]
    for_solvers(
        lambda m, t: remote(hmat.at[m], hs.at[me], sem_sh, sem_rh, t).start(),
        lambda m: pltpu.make_async_copy(hmat.at[m], hs.at[me], sem_rh).start(),
    )
    for_solvers(
        lambda m, t: remote(srcb.at[m], srcs.at[me], sem_sc, sem_rc, t).start(),
        lambda m: pltpu.make_async_copy(srcb.at[m], srcs.at[me], sem_rc).start(),
    )

    zero = jnp.zeros((128, 128), BF16)

    together = 4

    def build_g(i, carry):
        for j in range(together):
            drain(lin.at[i * together + j], sem_lin.at[i * together + j])
            drain(gup.at[i * together + j], sem_g.at[i * together + j])
        for j in range(together):
            m = i * together + j
            for b in range(0, blocks, 2):
                at = slice(b * 128, (b + 2) * 128)
                both = jnp.concatenate(
                    [jnp.concatenate([lin[m, b], zero], 1), jnp.concatenate([zero, lin[m, b + 1]], 1)], 0
                )
                gup[m, :, at] = dot(gup[m, :, at], both).astype(BF16)
        return carry

    lax.fori_loop(0, 1, build_g, 0)
    lax.fori_loop(1, modes // together, build_g, 0)

    def transform(jobs):
        at = 0
        while at < chunk:
            width = min(256, chunk - at)
            here = slice(at, at + width)
            need = sorted({s for _, pairs in jobs for s in pairs})
            phys = {s: dot(tf[...], xr[s, :, :, :, here].reshape(2 * M, width)) for s in need}
            for comp, (a, b, c, d) in jobs:
                crossed = phys[a] * phys[b] - phys[c] * phys[d]
                back = dot(tb[...], crossed.astype(BF16)).astype(BF16)
                nb[comp, :, :, :, here] = back.reshape(parts, 2, modes, width)
            at += width

    def give_back(group, comp):
        for d in (2, 3, 1):
            other = lax.rem(y + d, parts)
            to_mode(
                nb.at[comp, other], nr.at[comp, :, :, lanes_of(y)],
                sem_s2.at[group, d - 1], sem_r2.at[group, d - 1], other,
            ).start()
        nr[comp, :, :, lanes_of(y)] = nb[comp, y]

    exchanged(0, 0, 4)
    transform([(1, (VZ, BR, VR, BZ))])
    give_back(0, 1)

    mode_of = lax.rem(lax.broadcasted_iota(jnp.int32, (2 * modes, 128), 0), modes)
    leaf_update = jnp.zeros((2 * modes, 128), F32)
    for d in (0, 3, 1, 2):
        here = lanes_of(lax.rem(y + parts - d, parts))
        if d:
            drain(nb.at[1, 0], sem_r2.at[0, d - 1])
        source = stage[BP, :, :, here] + DT * nr[1, :, :, here].astype(F32)
        own = source.astype(BF16).reshape(2 * modes, chunk)
        src16[:, here] = own

        def update(m, acc, own=own, here=here):
            return acc + jnp.where(mode_of == m, dot_nt(own, gup[m, :, here]), 0.0)

        leaf_update = lax.fori_loop(0, modes, update, leaf_update, unroll=True)
        if d == 1:
            exchange(1, 4, 6)
    nl32[1] = nr[1].astype(F32)
    urow[...] = dot(leaf_update.astype(BF16), pt0[...])
    for m in range(modes):
        for c in range(2):
            ubuf[m, c : c + 1, :] = urow[c * modes + m : c * modes + m + 1, :]
    for_solvers(
        lambda m, t: remote(ubuf.at[m], us.at[me], sem_us, sem_ur, t).start(),
        lambda m: pltpu.make_async_copy(ubuf.at[m], us.at[me], sem_ur).start(),
    )

    def pair_at(b):
        return pl.ds(pl.multiple_of(b * 256, 256), 256)

    low = lax.broadcasted_iota(jnp.int32, (2 * modes, 256), 1) < 128

    def leaf_forward(b, carry):
        own = src16[:, pair_at(b)].astype(F32)
        own = jnp.concatenate([jnp.where(low, own, 0.0), jnp.where(low, 0.0, own)], 0).astype(BF16)
        left = right = jnp.zeros((2 * modes, 128), F32)
        for m in range(modes):
            got = dot_nt(own, jnp.concatenate([lin[m, 2 * b], lin[m, 2 * b + 1]], 1))
            left = jnp.where(mode_of == m, got[: 2 * modes], left)
            right = jnp.where(mode_of == m, got[2 * modes :], right)
        ls[:, pair_at(b)] = jnp.concatenate([left, right], 1).astype(BF16)
        return carry

    lax.fori_loop(0, blocks // 2, leaf_forward, 0, unroll=2)

    exchanged(1, 4, 6)
    transform([(0, (VP, BZ, VZ, BP)), (2, (VR, BP, VP, BR))])
    give_back(1, 0)
    give_back(2, 2)

    @pl.when(solver)
    def _():
        drain(hs, sem_rh)
        drain(srcs, sem_rc)
        drain(us, sem_ur)
        drain(ss, sem_rs)
        ranked = [[q for q in range(places) if level_of(q, levels) == k] for k in range(levels + 2)]
        top = places // 2
        none = jnp.zeros((2, 128), F32)

        def side(a, b):
            return jnp.concatenate([a, b], 1)

        def g_of(q, arrived):
            return srcs[q] - arrived

        joined = dot(ss[0], hs[top]).astype(BF16)
        g, w, x = {}, {}, {}
        arrived = {q: us[q - 1] + us[q] for q in ranked[1]}
        for level in range(1, levels):
            for q in ranked[level]:
                g[q] = g_of(q, arrived[q])
            for a, b in zip(ranked[level][::2], ranked[level][1::2]):
                both = side(g[a], g[b]).astype(BF16)
                arrived[(a + b) // 2] = dot_nt(both, side(hs[a], hs[b]))
            for a, b in zip(ranked[level][::2], ranked[level][1::2]):
                rows_ab = jnp.concatenate([side(g[a], none), side(none, g[b])], 0).astype(BF16)
                reduced = dot_nt(rows_ab, side(ss[a], ss[b])).astype(BF16)
                got = dot(reduced, side(ss[a], ss[b]))
                w[a], w[b] = got[:2, :128], got[2:, 128:]
        g_top = g_of(top, arrived[top]).astype(BF16)
        reduced_top = dot_nt(g_top, ss[top]).astype(BF16).astype(F32)
        reduced_0 = (dot_nt(srcs[0].astype(BF16), ss[0]) - dot_nt(g_top, joined)).astype(BF16)
        x[top] = dot(
            side(reduced_top, -reduced_0.astype(F32)).astype(BF16), jnp.concatenate([ss[top], joined], 0)
        )
        x[0] = dot(reduced_0, ss[0])
        for level in range(levels - 1, 0, -1):
            for a, b in zip(ranked[level][::2], ranked[level][1::2]):
                got = dot(x[parent_of(a, levels)].astype(BF16), side(hs[a], hs[b]))
                x[a], x[b] = w[a] - got[:, :128], w[b] - got[:, 128:]
        for p in range(places):
            xo[p, 0:2, :] = x[p]
            xo[p, 2:4, :] = x[2 * (p // 2) + 1]

        def send(p, carry):
            def away():
                pltpu.make_async_remote_copy(
                    src_ref=xo.at[p], dst_ref=xin.at[lax.div(me, 2)], send_sem=sem_xs, recv_sem=sem_xr,
                    device_id=(y, p), device_id_type=MESH,
                ).start()

            pl.when(p != me)(away)
            pl.when(p == me)(lambda: pltpu.make_async_copy(xo.at[p], xin.at[lax.div(me, 2)], sem_xr).start())
            return carry

        lax.fori_loop(0, places, send, 0)

    mode_col = jnp.concatenate([mode_of, mode_of], 0)

    def stacked(rows, which):
        rows = rows.astype(F32)
        return jnp.concatenate([jnp.where(which == m, rows, 0.0).astype(BF16) for m in range(modes)], 1)

    def leaf_back(b, carry):
        own = ls[:, pair_at(b)]
        own = stacked(jnp.concatenate([own[:, :128], own[:, 128:]], 0), mode_col)
        both = jnp.concatenate(
            [jnp.concatenate([lin[m, 2 * b], lin[m, 2 * b + 1]], 1) for m in range(modes)], 0
        )
        got = dot(own, both)
        az[:, pair_at(b)] = jnp.concatenate([got[: 2 * modes, :128], got[2 * modes :, 128:]], 1)
        return carry

    lax.fori_loop(0, blocks // 2, leaf_back, 0, unroll=5)

    for comp in (0, 2):
        for d in range(1, parts):
            drain(nb.at[comp, 0], sem_r2.at[1 + comp // 2, d - 1])
        nl32[comp] = nr[comp].astype(F32)

    for group, (lo, hi) in enumerate(((0, 4), (4, 6))):
        for d in range(1, parts):
            drain(xr.at[lo:hi, 0], sem_s1.at[group, d - 1])
    for group in range(3):
        for d in range(1, parts):
            drain(nb.at[0, 0], sem_s2.at[group, d - 1])

    def sent(count):
        drain(hmat.at[:count], sem_sh)
        drain(smat.at[:count], sem_ss)
        drain(srcb.at[:count], sem_sc)
        drain(ubuf.at[:count], sem_us)

    @pl.when(solver)
    def _():
        sent(modes - 1)
        drain(xo.at[: places - 1], sem_xs)

    pl.when(jnp.logical_not(solver))(lambda: sent(modes))

    drain(xin, sem_xr)
    for m in range(modes):
        for c in range(2):
            sol[c, m : m + 1, :] = xin[m, c : c + 1, :]
            urow[c * modes + m : c * modes + m + 1, :] = xin[m, 2 + c : 3 + c, :]
    above = dot_nt(urow[...].astype(BF16), pt0[...]).astype(BF16)

    above = stacked(above, mode_of)
    for b in range(blocks // 2):
        at = slice(b * 256, (b + 1) * 256)
        az[:, at] -= dot(above, gup[:, :, at].reshape(modes * 128, 256))


def put_out(*refs):
    moves = [pltpu.make_async_copy(refs[i], refs[3 + i], refs[6].at[i]) for i in range(3)]
    for move in moves:
        move.start()
    for move in moves:
        move.wait()


def solution(mesh):
    parts, places = mesh.shape["mode"], mesh.shape["mesh"]
    in_specs = (
        P(None, None, "mode", "mesh"),
        P(None, None, "mode", "mesh"),
        P("mode", "mesh", None, None),
        P("mode", None, "mesh"),
        P("mode", "mesh", None),
        P("mode", "mesh", None),
        P(None, "mode", "mesh"),
        P("mesh", None, None),
    )
    out_specs = (P(None, None, "mode", "mesh"), P(None, "mode", "mesh"), P(None, "mode", "mesh"))

    def shards(vel, mag, linv, lcpl, sinv, scpl, ssrc, rows):
        modes, nodes = vel.shape[2], vel.shape[3]
        blocks = linv.shape[1]
        chunk = nodes // parts
        tab_f, tab_b = tables(parts)
        vm = pltpu.VMEM
        dma = pltpu.SemaphoreType.DMA
        scratch = [
            vm((6, 2, modes, nodes), F32),
            vm((6, 2, modes, nodes), BF16),
            vm((6, parts, 2, modes, chunk), BF16),
            vm((NPHI, 2 * M), BF16),
            vm((2 * M, NPHI), BF16),
            vm((3, parts, 2, modes, chunk), BF16),
            vm((3, 2, modes, nodes), BF16),
            vm((2 * modes, nodes), BF16),
            vm((modes, blocks, 128, 128), BF16),
            vm((modes, 128, nodes), BF16),
            vm((modes, 128, 128), BF16),
            vm((modes, 128, 128), BF16),
            vm((modes, 128, 128), BF16),
            vm((2, modes, 128), F32),
            vm((1, 2, 128), jnp.int32),
            vm((128, 128), BF16),
            vm((128, 128), BF16),
            vm((modes, 2, 128), F32),
            vm((modes, 2, 128), F32),
            vm((2 * modes, 128), F32),
            vm((places, 128, 128), BF16),
            vm((places, 128, 128), BF16),
            vm((places, 2, 128), F32),
            vm((places, 2, 128), F32),
            vm((places, 4, 128), F32),
            vm((modes, 4, 128), F32),
            vm((2 * modes, nodes), BF16),
            dma((6,)), dma((6,)), dma((modes,)), dma((modes,)),
            dma((2, parts - 1)), dma((2, parts - 1)),
            dma((3, parts - 1)), dma((3, parts - 1)),
            dma, dma, dma, dma, dma, dma, dma, dma, dma, dma,
        ]
        any_spec = pl.BlockSpec(memory_space=pl.ANY)

        def body(*refs):
            kernel(parts, places, *refs)

        shapes = ((3, 2, modes, nodes), (2 * modes, nodes), (2, modes, 128))
        held = pl.pallas_call(
            body,
            name="dynamo",
            out_shape=tuple(pltpu.VMEM(shape, F32) for shape in shapes),
            in_specs=[any_spec] * 10,
            out_specs=(pl.BlockSpec(memory_space=pltpu.VMEM),) * 3,
            scratch_shapes=scratch,
            compiler_params=pltpu.CompilerParams(
                collective_id=0, has_side_effects=True, vmem_limit_bytes=65_650_000
            ),
        )(vel, mag, linv, lcpl, sinv, scpl, ssrc, rows, tab_f, tab_b)
        nl, az, sol = pl.pallas_call(
            put_out,
            name="put_out",
            out_shape=tuple(jax.ShapeDtypeStruct(shape, F32) for shape in shapes),
            in_specs=[pl.BlockSpec(memory_space=pltpu.VMEM)] * 3,
            out_specs=(any_spec,) * 3,
            scratch_shapes=[dma((3,))],
            compiler_params=pltpu.CompilerParams(has_side_effects=True, vmem_limit_bytes=60 * 2**20),
        )(*[pltpu.with_memory_space_constraint(a, pltpu.VMEM) for a in held])
        return nl, az.reshape(2, modes, nodes), sol

    return jax.shard_map(shards, mesh=mesh, in_specs=in_specs, out_specs=out_specs, check_vma=False)
```

time: 56.3 us -> 41.8 us (0.74)
  Pallas kernels: 50.1 us -> 41.1 us
  local copies, waits for them, and re-layouts: 5.25 us -> 0 us
    pallas_call x1 -> x2, Pallas kernels: 50.1 us -> 41.1 us  [the longest x1 40 us: shards(): pl.pallas_call(body, name='dynamo', out_shape=tuple((pltpu.VMEM(shape, F3...]
    unnamed x3 -> x0, local copies, waits for them, and re-layouts: 5.25 us -> none
where the time goes in v2:
time: 41.8 us; the launch traced here: 41.7 us
  Pallas kernels  41.1 us (98%)
  between operations  0.64 us (2%)
    pallas_call x1, Pallas kernels, shards(): pl.pallas_call(body, name='dynamo', out_shape=tuple((pltpu.VMEM(shape, F3...  40 us
    pallas_call x1, Pallas kernels, shards(): pl.pallas_call(put_out, name='put_out', out_shape=tuple((jax.ShapeDtypeSt...  1.08 us

profile of v2, /device:TPU:1, one launch (start us, length us, event | category | flops | bytes accessed | tf_op | source)
XLA Modules:
  0.0 41.7 jit_solution(15468931426526224376)
XLA Ops:
  0.6 40.0 %dynamo.1 = (f32[3,2,16,2560]{3,2,1,0:T(8,128)S(1)}, f32[32,2560]{1,0:T(8,128)S(1)}, f32[2,16,128]{2,1,0:T(8,128)S(1)}) custom-call(f32[3,2,16,2560]{3,2,1,0:T(8,128)} %refs_0_.1, f32[3,2,16,2560]{3,2,1,0:T(8,128)} %refs_1_.1, bf16[16,20,128,128]{3,2,1,0:T(8,128)(2,1)} %refs_2_.1, bf16[16,128,2560]{2,1,0:T(8,128)(2,1)} %refs_3_.1, ...), custom_call_target="tpu_custom_call" | custom-call | tf_op jit(solution)/shard_map/dynamo/pallas_call | solution.py:453
  40.6 1.1 %put_out.1 = (f32[3,2,16,2560]{3,2,1,0:T(8,128)}, f32[32,2560]{1,0:T(8,128)}, f32[2,16,128]{2,1,0:T(8,128)}) custom-call(f32[3,2,16,2560]{3,2,1,0:T(8,128)S(1)} %get-tuple-element.9.refs_0_, f32[32,2560]{1,0:T(8,128)S(1)} %get-tuple-element.10.refs_1_, f32[2,16,128]{2,1,0:T(8,128)S(1)} %get-tuple-element.11.refs_2_), custom_call_target="tpu_custom_call" | custom-call | tf_op jit(solution)/shard_map/put_out/pallas_call | solution.py:464

commit v3 on v2

--- a/solution.py
+++ b/solution.py
@@ -52,7 +52,7 @@
     parts, places,
     vel, mag, linv, lcpl, sinv, scpl, ssrc, rows, tab_f, tab_b,
     nl32, az, sol,
-    stage, vb, xr, tf, tb, nb, nr, src16, lin, gup, smat, cmat, hmat, ssv, rowv, pt0, p1,
+    stage, vb, xr, tf, tb, nb, nr, src16, lin, gup, gt, smat, cmat, hmat, ssv, rowv, pt0, p1,
     srcb, ubuf, urow, hs, ss, srcs, us, xo, xin, ls,
     sem_vb, sem_small, sem_lin, sem_g, sem_s1, sem_r1, sem_s2, sem_r2,
     sem_ss, sem_sh, sem_sc, sem_rs, sem_rh, sem_rc, sem_us, sem_ur, sem_xs, sem_xr,
@@ -65,6 +65,7 @@
     y = lax.axis_index("mode")
     me = lax.axis_index("mesh")
     solver = lax.rem(me, 2) == 1
+    together = 4
 
     def lanes_of(part):
         return pl.ds(pl.multiple_of(part * chunk, 128), chunk)
@@ -73,7 +74,7 @@
         pltpu.make_async_copy(ref, ref, sem).wait()
 
     for slot, (which, comp) in enumerate(SLOT_OF):
-        pltpu.make_async_copy((vel, mag)[which].at[comp], stage.at[slot], sem_vb.at[slot]).start()
+        pltpu.make_async_copy((vel, mag)[which].at[comp], stage.at[slot], sem_vb.at[slot // 4]).start()
     barrier = pltpu.get_barrier_semaphore()
 
     def greet(i, carry):
@@ -89,24 +90,35 @@
     for i, (a, b) in enumerate(small):
         pltpu.make_async_copy(a, b, sem_small.at[i]).start()
 
+    drain(stage.at[:4], sem_vb.at[0])
     for slot in range(4):
-        drain(stage.at[slot], sem_vb.at[slot])
         vb[slot] = stage[slot].astype(BF16)
+    for i, (a, b) in enumerate(small):
+        drain(b, sem_small.at[i])
+
+    srow = lax.broadcasted_iota(jnp.int32, (128, 128), 0)
+    pt0[...] = (srow == jnp.broadcast_to(rowv[0, 0:1, :], (128, 128))).astype(F32).astype(BF16)
+    p1[...] = (srow == jnp.broadcast_to(rowv[0, 1:2, :], (128, 128))).astype(F32).T.astype(BF16)
+
+    def build_h(m, carry):
+        coupling = dot(p1[...], cmat[m]).astype(BF16)
+        hmat[m] = dot(coupling, smat[m]).astype(BF16)
+        return carry
+
+    lax.fori_loop(0, modes // 4 * 3, build_h, 0, unroll=4)
     pl.semaphore_wait(barrier, parts - 1 + places - 1)
 
     def to_mode(src, dst, send, recv, other):
         return pltpu.make_async_remote_copy(
             src_ref=src, dst_ref=dst, send_sem=send, recv_sem=recv, device_id=(other, me), device_id_type=MESH
         )
-
-    after, before = lax.rem(y + 1, parts), lax.rem(y + parts - 1, parts)
 
     def exchange(group, lo, hi):
         for d in (2, 3, 1):
             other = lax.rem(y + d, parts)
             to_mode(
                 vb.at[lo:hi, :, :, lanes_of(other)], xr.at[lo:hi, y],
-                sem_s1.at[group, d - 1], sem_r1.at[group, d - 1], other,
+                sem_s1.at[group], sem_r1.at[group, d - 1], other,
             ).start()
         for slot in range(lo, hi):
             xr[slot, y] = vb[slot, :, :, lanes_of(y)]
@@ -116,19 +128,17 @@
             drain(xr.at[lo:hi, 0], sem_r1.at[group, d - 1])
 
     exchange(0, 0, 4)
+
     def load_mode(m, carry):
-        pltpu.make_async_copy(linv.at[m], lin.at[m], sem_lin.at[m]).start()
-        pltpu.make_async_copy(lcpl.at[m], gup.at[m], sem_g.at[m]).start()
+        pltpu.make_async_copy(linv.at[m], lin.at[m], sem_lin.at[lax.div(m, together)]).start()
+        pltpu.make_async_copy(lcpl.at[m], gup.at[m], sem_g.at[lax.div(m, together)]).start()
         return carry
 
     lax.fori_loop(0, modes, load_mode, 0)
 
+    drain(stage.at[4:], sem_vb.at[1])
     for slot in range(4, 6):
-        drain(stage.at[slot], sem_vb.at[slot])
         vb[slot] = stage[slot].astype(BF16)
-
-    for i, (a, b) in enumerate(small):
-        drain(b, sem_small.at[i])
 
     def for_solvers(act, own):
         def one(m, carry):
@@ -137,27 +147,18 @@
             pl.when(there == me)(lambda: own(m))
             return carry
 
-        lax.fori_loop(0, modes, one, 0)
+        lax.fori_loop(0, modes, one, 0, unroll=4)
 
     def remote(src, dst, send, recv, there):
         return pltpu.make_async_remote_copy(
             src_ref=src, dst_ref=dst, send_sem=send, recv_sem=recv, device_id=(y, there), device_id_type=MESH
         )
 
+    lax.fori_loop(modes // 4 * 3, modes, build_h, 0, unroll=4)
     for_solvers(
         lambda m, t: remote(smat.at[m], ss.at[me], sem_ss, sem_rs, t).start(),
         lambda m: pltpu.make_async_copy(smat.at[m], ss.at[me], sem_rs).start(),
     )
-    srow = lax.broadcasted_iota(jnp.int32, (128, 128), 0)
-    pt0[...] = (srow == jnp.broadcast_to(rowv[0, 0:1, :], (128, 128))).astype(F32).astype(BF16)
-    p1[...] = (srow == jnp.broadcast_to(rowv[0, 1:2, :], (128, 128))).astype(F32).T.astype(BF16)
-
-    def build_h(m, carry):
-        coupling = dot(p1[...], cmat[m]).astype(BF16)
-        hmat[m] = dot(coupling, smat[m]).astype(BF16)
-        return carry
-
-    lax.fori_loop(0, modes, build_h, 0, unroll=4)
     srcb[...] = jnp.zeros_like(srcb)
     ubuf[...] = jnp.zeros_like(ubuf)
     for m in range(modes):
@@ -174,12 +175,10 @@
 
     zero = jnp.zeros((128, 128), BF16)
 
-    together = 4
-
     def build_g(i, carry):
-        for j in range(together):
-            drain(lin.at[i * together + j], sem_lin.at[i * together + j])
-            drain(gup.at[i * together + j], sem_g.at[i * together + j])
+        these = pl.ds(i * together, together)
+        drain(lin.at[these], sem_lin.at[i])
+        drain(gup.at[these], sem_g.at[i])
         for j in range(together):
             m = i * together + j
             for b in range(0, blocks, 2):
@@ -187,7 +186,9 @@
                 both = jnp.concatenate(
                     [jnp.concatenate([lin[m, b], zero], 1), jnp.concatenate([zero, lin[m, b + 1]], 1)], 0
                 )
-                gup[m, :, at] = dot(gup[m, :, at], both).astype(BF16)
+                made = dot(gup[m, :, at], both).astype(BF16)
+                gup[m, :, at] = made
+                gt[i * (together // 2) + j // 2, at, (j % 2) * 128 : (j % 2 + 1) * 128] = made.T
         return carry
 
     lax.fori_loop(0, 1, build_g, 0)
@@ -211,7 +212,7 @@
             other = lax.rem(y + d, parts)
             to_mode(
                 nb.at[comp, other], nr.at[comp, :, :, lanes_of(y)],
-                sem_s2.at[group, d - 1], sem_r2.at[group, d - 1], other,
+                sem_s2.at[group], sem_r2.at[group, d - 1], other,
             ).start()
         nr[comp, :, :, lanes_of(y)] = nb[comp, y]
 
@@ -229,10 +230,10 @@
         own = source.astype(BF16).reshape(2 * modes, chunk)
         src16[:, here] = own
 
-        def update(m, acc, own=own, here=here):
-            return acc + jnp.where(mode_of == m, dot_nt(own, gup[m, :, here]), 0.0)
-
-        leaf_update = lax.fori_loop(0, modes, update, leaf_update, unroll=True)
+        for i in range(modes // 2):
+            got = dot(own, gt[i, here, :])
+            for j in range(2):
+                leaf_update += jnp.where(mode_of == 2 * i + j, got[:, j * 128 : (j + 1) * 128], 0.0)
         if d == 1:
             exchange(1, 4, 6)
     nl32[1] = nr[1].astype(F32)
@@ -287,28 +288,43 @@
         joined = dot(ss[0], hs[top]).astype(BF16)
         g, w, x = {}, {}, {}
         arrived = {q: us[q - 1] + us[q] for q in ranked[1]}
+        reduced = {}
+
+        def pairs(level):
+            return list(zip(ranked[level][::2], ranked[level][1::2]))
+
+        def up(level):
+            for a, b in pairs(level):
+                g[a], g[b] = g_of(a, arrived[a]), g_of(b, arrived[b])
+                arrived[(a + b) // 2] = dot_nt(side(g[a], g[b]).astype(BF16), side(hs[a], hs[b]))
+
+        def reduce_pairs(level):
+            for a, b in pairs(level):
+                rows_ab = jnp.concatenate([side(g[a], none), side(none, g[b])], 0).astype(BF16)
+                reduced[a] = dot_nt(rows_ab, side(ss[a], ss[b])).astype(BF16)
+
+        def back_pairs(level):
+            for a, b in pairs(level):
+                got = dot(reduced[a], side(ss[a], ss[b]))
+                w[a], w[b] = got[:2, :128], got[2:, 128:]
+
         for level in range(1, levels):
-            for q in ranked[level]:
-                g[q] = g_of(q, arrived[q])
-            for a, b in zip(ranked[level][::2], ranked[level][1::2]):
-                both = side(g[a], g[b]).astype(BF16)
-                arrived[(a + b) // 2] = dot_nt(both, side(hs[a], hs[b]))
-            for a, b in zip(ranked[level][::2], ranked[level][1::2]):
-                rows_ab = jnp.concatenate([side(g[a], none), side(none, g[b])], 0).astype(BF16)
-                reduced = dot_nt(rows_ab, side(ss[a], ss[b])).astype(BF16)
-                got = dot(reduced, side(ss[a], ss[b]))
-                w[a], w[b] = got[:2, :128], got[2:, 128:]
+            up(level)
+            if level > 1:
+                back_pairs(level - 1)
+            reduce_pairs(level)
         g_top = g_of(top, arrived[top]).astype(BF16)
         reduced_top = dot_nt(g_top, ss[top]).astype(BF16).astype(F32)
         reduced_0 = (dot_nt(srcs[0].astype(BF16), ss[0]) - dot_nt(g_top, joined)).astype(BF16)
+        back_pairs(levels - 1)
         x[top] = dot(
             side(reduced_top, -reduced_0.astype(F32)).astype(BF16), jnp.concatenate([ss[top], joined], 0)
         )
-        x[0] = dot(reduced_0, ss[0])
         for level in range(levels - 1, 0, -1):
             for a, b in zip(ranked[level][::2], ranked[level][1::2]):
                 got = dot(x[parent_of(a, levels)].astype(BF16), side(hs[a], hs[b]))
                 x[a], x[b] = w[a] - got[:, :128], w[b] - got[:, 128:]
+        x[0] = dot(reduced_0, ss[0])
         for p in range(places):
             xo[p, 0:2, :] = x[p]
             xo[p, 2:4, :] = x[2 * (p // 2) + 1]
@@ -324,7 +340,7 @@
             pl.when(p == me)(lambda: pltpu.make_async_copy(xo.at[p], xin.at[lax.div(me, 2)], sem_xr).start())
             return carry
 
-        lax.fori_loop(0, places, send, 0)
+        lax.fori_loop(0, places, send, 0, unroll=8)
 
     mode_col = jnp.concatenate([mode_of, mode_of], 0)
 
@@ -344,17 +360,10 @@
 
     lax.fori_loop(0, blocks // 2, leaf_back, 0, unroll=5)
 
-    for comp in (0, 2):
-        for d in range(1, parts):
-            drain(nb.at[comp, 0], sem_r2.at[1 + comp // 2, d - 1])
-        nl32[comp] = nr[comp].astype(F32)
-
     for group, (lo, hi) in enumerate(((0, 4), (4, 6))):
-        for d in range(1, parts):
-            drain(xr.at[lo:hi, 0], sem_s1.at[group, d - 1])
+        drain(xr.at[lo:hi, : parts - 1], sem_s1.at[group])
     for group in range(3):
-        for d in range(1, parts):
-            drain(nb.at[0, 0], sem_s2.at[group, d - 1])
+        drain(nb.at[0, : parts - 1], sem_s2.at[group])
 
     def sent(count):
         drain(hmat.at[:count], sem_sh)
@@ -372,7 +381,6 @@
     drain(xin, sem_xr)
     for m in range(modes):
         for c in range(2):
-            sol[c, m : m + 1, :] = xin[m, c : c + 1, :]
             urow[c * modes + m : c * modes + m + 1, :] = xin[m, 2 + c : 3 + c, :]
     above = dot_nt(urow[...].astype(BF16), pt0[...]).astype(BF16)
 
@@ -380,6 +388,13 @@
     for b in range(blocks // 2):
         at = slice(b * 256, (b + 1) * 256)
         az[:, at] -= dot(above, gup[:, :, at].reshape(modes * 128, 256))
+    for comp in (0, 2):
+        for d in range(1, parts):
+            drain(nb.at[comp, 0], sem_r2.at[1 + comp // 2, d - 1])
+        nl32[comp] = nr[comp].astype(F32)
+    for m in range(modes):
+        for c in range(2):
+            sol[c, m : m + 1, :] = xin[m, c : c + 1, :]
 
 
 def put_out(*refs):
@@ -422,6 +437,7 @@
             vm((2 * modes, nodes), BF16),
             vm((modes, blocks, 128, 128), BF16),
             vm((modes, 128, nodes), BF16),
+            vm((modes // 2, nodes, 256), BF16),
             vm((modes, 128, 128), BF16),
             vm((modes, 128, 128), BF16),
             vm((modes, 128, 128), BF16),
@@ -439,9 +455,9 @@
             vm((places, 4, 128), F32),
             vm((modes, 4, 128), F32),
             vm((2 * modes, nodes), BF16),
-            dma((6,)), dma((6,)), dma((modes,)), dma((modes,)),
-            dma((2, parts - 1)), dma((2, parts - 1)),
-            dma((3, parts - 1)), dma((3, parts - 1)),
+            dma((2,)), dma((6,)), dma((4,)), dma((4,)),
+            dma((2,)), dma((2, parts - 1)),
+            dma((3,)), dma((3, parts - 1)),
             dma, dma, dma, dma, dma, dma, dma, dma, dma, dma,
         ]
         any_spec = pl.BlockSpec(memory_space=pl.ANY)

time: 41.8 us -> 38.5 us (0.921)
  Pallas kernels: 41.1 us -> 37.7 us
    pallas_call x1, Pallas kernels: 40 us -> 36.6 us  [shards(): pl.pallas_call(body, name='dynamo', out_shape=tuple((pltpu.VMEM(shape, F3...]
where the time goes in v3:
time: 38.5 us; the launch traced here: 38.4 us
  Pallas kernels  37.7 us (98%)
  between operations  0.64 us (2%)
    pallas_call x1, Pallas kernels, shards(): pl.pallas_call(body, name='dynamo', out_shape=tuple((pltpu.VMEM(shape, F3...  36.6 us
    pallas_call x1, Pallas kernels, shards(): pl.pallas_call(put_out, name='put_out', out_shape=tuple((jax.ShapeDtypeSt...  1.08 us

profile of v3, /device:TPU:1, one launch (start us, length us, event | category | flops | bytes accessed | tf_op | source)
XLA Modules:
  0.0 38.4 jit_solution(15929167564916858566)
XLA Ops:
  0.6 36.6 %dynamo.1 = (f32[3,2,16,2560]{3,2,1,0:T(8,128)S(1)}, f32[32,2560]{1,0:T(8,128)S(1)}, f32[2,16,128]{2,1,0:T(8,128)S(1)}) custom-call(f32[3,2,16,2560]{3,2,1,0:T(8,128)} %refs_0_.1, f32[3,2,16,2560]{3,2,1,0:T(8,128)} %refs_1_.1, bf16[16,20,128,128]{3,2,1,0:T(8,128)(2,1)} %refs_2_.1, bf16[16,128,2560]{2,1,0:T(8,128)(2,1)} %refs_3_.1, ...), custom_call_target="tpu_custom_call" | custom-call | tf_op jit(solution)/shard_map/dynamo/pallas_call | solution.py:469
  37.3 1.1 %put_out.1 = (f32[3,2,16,2560]{3,2,1,0:T(8,128)}, f32[32,2560]{1,0:T(8,128)}, f32[2,16,128]{2,1,0:T(8,128)}) custom-call(f32[3,2,16,2560]{3,2,1,0:T(8,128)S(1)} %get-tuple-element.9.refs_0_, f32[32,2560]{1,0:T(8,128)S(1)} %get-tuple-element.10.refs_1_, f32[2,16,128]{2,1,0:T(8,128)S(1)} %get-tuple-element.11.refs_2_), custom_call_target="tpu_custom_call" | custom-call | tf_op jit(solution)/shard_map/put_out/pallas_call | solution.py:480

commit v4 on v3

--- a/solution.py
+++ b/solution.py
@@ -77,14 +77,17 @@
         pltpu.make_async_copy((vel, mag)[which].at[comp], stage.at[slot], sem_vb.at[slot // 4]).start()
     barrier = pltpu.get_barrier_semaphore()
 
-    def greet(i, carry):
-        other = jnp.where(me + i >= places, me + i - places, me + i)
+    def around(at, step, size):
+        return jnp.where(at + step >= size, at + step - size, at + step)
+
+    def far_first(size):
+        return sorted(range(1, size), key=lambda i: -min(i, size - i))
+
+    for step in far_first(places):
+        other = around(me, step, places)
         pl.semaphore_signal(barrier, inc=1, device_id=(y, other), device_id_type=MESH)
-        return carry
-
     for d in range(1, parts):
         pl.semaphore_signal(barrier, inc=1, device_id=(lax.rem(y + d, parts), me), device_id_type=MESH)
-    lax.fori_loop(1, places, greet, 0)
 
     small = ((sinv, smat), (scpl, cmat), (ssrc, ssv), (rows, rowv), (tab_f, tf), (tab_b, tb))
     for i, (a, b) in enumerate(small):
@@ -141,13 +144,12 @@
         vb[slot] = stage[slot].astype(BF16)
 
     def for_solvers(act, own):
-        def one(m, carry):
-            there = 2 * m + 1
-            pl.when(there != me)(lambda: act(m, there))
-            pl.when(there == me)(lambda: own(m))
-            return carry
-
-        lax.fori_loop(0, modes, one, 0, unroll=4)
+        chip = lax.div(me, 2)
+        for step in far_first(modes):
+            m = around(chip, step, modes)
+            act(m, 2 * m + 1)
+        pl.when(solver)(lambda: own(chip))
+        pl.when(jnp.logical_not(solver))(lambda: act(chip, me + 1))
 
     def remote(src, dst, send, recv, there):
         return pltpu.make_async_remote_copy(
@@ -329,18 +331,11 @@
             xo[p, 0:2, :] = x[p]
             xo[p, 2:4, :] = x[2 * (p // 2) + 1]
 
-        def send(p, carry):
-            def away():
-                pltpu.make_async_remote_copy(
-                    src_ref=xo.at[p], dst_ref=xin.at[lax.div(me, 2)], send_sem=sem_xs, recv_sem=sem_xr,
-                    device_id=(y, p), device_id_type=MESH,
-                ).start()
-
-            pl.when(p != me)(away)
-            pl.when(p == me)(lambda: pltpu.make_async_copy(xo.at[p], xin.at[lax.div(me, 2)], sem_xr).start())
-            return carry
-
-        lax.fori_loop(0, places, send, 0, unroll=8)
+        mine = lax.div(me, 2)
+        for step in far_first(places):
+            p = around(me, step, places)
+            remote(xo.at[p], xin.at[mine], sem_xs, sem_xr, p).start()
+        pltpu.make_async_copy(xo.at[me], xin.at[mine], sem_xr).start()
 
     mode_col = jnp.concatenate([mode_of, mode_of], 0)
 

time: 38.5 us -> 38.3 us (level)
  no operation moved by 1% of the time
where the time goes in v4:
time: 38.3 us; the launch traced here: 38.2 us
  Pallas kernels  37.6 us (98%)
  between operations  0.64 us (2%)
    pallas_call x1, Pallas kernels, shards(): pl.pallas_call(body, name='dynamo', out_shape=tuple((pltpu.VMEM(shape, F3...  36.5 us
    pallas_call x1, Pallas kernels, shards(): pl.pallas_call(put_out, name='put_out', out_shape=tuple((jax.ShapeDtypeSt...  1.08 us

profile of v4, /device:TPU:1, one launch (start us, length us, event | category | flops | bytes accessed | tf_op | source)
XLA Modules:
  0.0 38.2 jit_solution(12022722404730659445)
XLA Ops:
  0.6 36.5 %dynamo.1 = (f32[3,2,16,2560]{3,2,1,0:T(8,128)S(1)}, f32[32,2560]{1,0:T(8,128)S(1)}, f32[2,16,128]{2,1,0:T(8,128)S(1)}) custom-call(f32[3,2,16,2560]{3,2,1,0:T(8,128)} %refs_0_.1, f32[3,2,16,2560]{3,2,1,0:T(8,128)} %refs_1_.1, bf16[16,20,128,128]{3,2,1,0:T(8,128)(2,1)} %refs_2_.1, bf16[16,128,2560]{2,1,0:T(8,128)(2,1)} %refs_3_.1, ...), custom_call_target="tpu_custom_call" | custom-call | tf_op jit(solution)/shard_map/dynamo/pallas_call | solution.py:464
  37.1 1.1 %put_out.1 = (f32[3,2,16,2560]{3,2,1,0:T(8,128)}, f32[32,2560]{1,0:T(8,128)}, f32[2,16,128]{2,1,0:T(8,128)}) custom-call(f32[3,2,16,2560]{3,2,1,0:T(8,128)S(1)} %get-tuple-element.9.refs_0_, f32[32,2560]{1,0:T(8,128)S(1)} %get-tuple-element.10.refs_1_, f32[2,16,128]{2,1,0:T(8,128)S(1)} %get-tuple-element.11.refs_2_), custom_call_target="tpu_custom_call" | custom-call | tf_op jit(solution)/shard_map/put_out/pallas_call | solution.py:475
